TPU v7x, 256 devices: a whole 4x4x8 slice. The times are simulated.
256 devices in a mesh: gx: 8 (over y, x_lo), gy: 4 (over x_hi, core), gz: 8 (over z).
Axes of the slice: x: 4 (x_hi: 2, x_lo: 2; x = x_hi * 2 + x_lo), y: 4, z: 8, core: 2. Of those that a mesh axis runs over, the one named last changes fastest.
Arguments:
- occupancy: int32 [128, 256, 1024], P('gx', 'gy', 'gz'), may hold values 0 or 1
- site_field: float32 [128, 256, 1024], P('gx', 'gy', 'gz'), may hold values from -6 to 6
- attempt_rate: float32 [128, 256, 1024], P('gx', 'gy', 'gz'), may hold values from 0.2 to 5
- uniforms: float32 [8, 128, 256, 512], P(None, 'gx', 'gy', 'gz'), may hold values from 0.001 to 1
Outputs:
- final_spins: float32 [128, 256, 1024], P('gx', 'gy', 'gz')
- history: float32 [2, 8], replicated
All inputs are finite; a program needn't handle non-finite values. No bound on the sum of `occupancy` on one device may be relied on, other than what follows from the above.
Results may differ from a plain program's by a relative error of at most 0.0002.
Values sent between devices are 32-bit elements; how exact they have to be, the bound alone decides.
No kernel may reach another device: no remote copies, remote signals or barrier semaphores. Data moves between devices by JAX's collectives and lax.ppermute only.
A program may use at most 128 MiB of HBM per device.

v0:
```python
import functools

import jax
import jax.numpy as jnp
from jax import lax
from jax.experimental import pallas as pl
from jax.experimental.pallas import tpu as pltpu
from jax.sharding import PartitionSpec as P


SECTIONS = 8
AXES = ("gx", "gy", "gz")
BX, BY, BZ = 16, 64, 128
HY, HZ = BY // 2, BZ // 2
UNROLL = 16
CHUNK = 4
PITCH = HY + 8
F32, BF16 = jnp.float32, jnp.bfloat16


def lane_of(rows=HY):
    return lax.broadcasted_iota(jnp.int32, (rows, BZ), 1)


def odd_row(shift, rows=HY):
    return (lax.broadcasted_iota(jnp.int32, (rows, BZ), 0) + shift) % 2 == 1


def roll(value, shift):
    shift = shift % BZ
    return value if shift == 0 else pltpu.roll(value, shift, 1)


def shuffle_matrix(transposed):
    major = lax.broadcasted_iota(jnp.int32, (BZ, BZ), 1 if transposed else 0)
    minor = lax.broadcasted_iota(jnp.int32, (BZ, BZ), 0 if transposed else 1)
    return (minor == major // 2 + HZ * (major % 2)).astype(F32)


def matmul(a, b, exact):
    precision = lax.Precision.HIGHEST if exact else lax.Precision.DEFAULT
    return jnp.dot(a, b, precision=precision, preferred_element_type=F32)


def add_face(column, plane, x, odd):
    slot = (2 * x - jnp.where(odd, 1, 0)) % HZ
    return jnp.where(lane_of() % HZ == slot, pltpu.roll(plane, 2 * x, 1), column)


def fetch(pairs, arrived):
    copies = [pltpu.make_async_copy(source, target, arrived.at[i]) for i, (source, target) in enumerate(pairs)]
    for copy in copies:
        copy.start()
    return copies


def split_sites(mixed, odd, low):
    lower, upper = mixed[:HY], mixed[HY:]
    lower_turned, upper_turned = roll(lower, HZ), roll(upper, HZ)
    even_site = jnp.where(low, jnp.where(odd, lower_turned, lower), jnp.where(odd, upper, upper_turned))
    odd_site = jnp.where(low, jnp.where(odd, lower, lower_turned), jnp.where(odd, upper_turned, upper))
    return even_site, odd_site


def spins_kernel(where, occ_hbm, spin, x_one, x_two, y_one, y_two, zed, occ, arrived):
    copies = fetch([(occ_hbm.at[pl.ds(c * CHUNK, CHUNK)], occ.at[pl.ds(c * CHUNK, CHUNK)]) for c in range(BX // CHUNK)], arrived)
    lane = lane_of()
    wide = shuffle_matrix(False)
    columns = [jnp.zeros((HY, BZ), F32)] * 2
    for x in range(BX):
        if x % CHUNK == 0:
            copies[x // CHUNK].wait()
        planes = split_sites(matmul(2.0 * occ[x].astype(F32) - 1.0, wide, False), odd_row(x), lane < HZ)
        for p, plane in enumerate(planes):
            spin[p, x + 1, :HY] = plane
            columns[p] = add_face(columns[p], plane, x, odd_row(x + p))
    for p in range(2):
        x_one[p] = spin[p, far_or_near(where[1], BX, 1), :HY]
        x_two[p] = spin[p, far_or_near(where[1], 1, BX), :HY]
        one, two = far_or_near(where[2], HY - 1, 0), far_or_near(where[2], 0, HY - 1)
        for x in range(BX):
            y_one[p, x : x + 1] = spin[p, x + 1, pl.ds(one, 1)]
            y_two[p, x : x + 1] = spin[p, x + 1, pl.ds(two, 1)]
        zed[p] = columns[p]


def shuffled(value, wide):
    high = value.astype(BF16)
    rest = value - high.astype(F32)
    middle = rest.astype(BF16)
    low = (rest - middle.astype(F32)).astype(BF16)
    rows = value.shape[0]
    parts = jnp.dot(jnp.concatenate([high, middle, low], axis=0), wide, preferred_element_type=F32)
    return parts[:rows] + parts[rows : 2 * rows] + parts[2 * rows :]


def fields_kernel(field_hbm, attempt_hbm, uniforms, h, a, v, field, attempt, raw, arrived):
    copies = fetch([(field_hbm, field), (attempt_hbm, attempt), (uniforms.at[0], raw)], arrived)
    low = lane_of() < HZ
    wide = shuffle_matrix(False).astype(BF16)
    for copy in copies:
        copy.wait()

    @pl.loop(0, BX // UNROLL)
    def _(i):
        for j in range(UNROLL):
            x = i * UNROLL + j
            h[0, x], h[1, x] = split_sites(shuffled(field[x], wide), odd_row(j), low)
            even_site, odd_site = split_sites(shuffled(attempt[x], wide), odd_row(j), low)
            a[0, x], a[1, x] = even_site, odd_site
            v[x] = merged(raw[x]) / even_site


def merged(draws):
    return jnp.concatenate([draws[:HY], draws[HY:]], axis=1)


def draw_kernel(act, where, uniforms, a, v, raw, arrived):
    (copy,) = fetch([(uniforms.at[where[0]], raw)], arrived)
    copy.wait()

    @pl.loop(0, BX // UNROLL)
    def _(i):
        for j in range(UNROLL):
            x = i * UNROLL + j
            v[x] = merged(raw[x]) / a[act, x]


def far_or_near(even, far, near):
    return jnp.where(even == 1, far, near)


def pick(even, first, second):
    return jnp.where(even == 1, first, second)


def side_halo(where, one, two):
    return jnp.where(lane_of(BX) < HZ, pick(where[2], one, two), pick(where[2], two, one))


def column_halo(where, one, two):
    return jnp.where(lane_of() % 2 == 1, pick(where[3], two, one), pick(where[3], one, two))


def flip_of(total, half):
    ratio = total / half
    square = ratio * ratio
    return lambda odds: 1.0 - 2.0 / (1.0 + odds * square)


def eighth(value):
    return value[0:8] + value[8:16] + value[16:24] + value[24:32]


def advance(k, p, half, gathered, halo, spin, side, column, odds, gain, h, energy, fields, clock):
    rows = gathered.shape[0]
    parts = gathered[...]
    while rows % 16 == 0:
        rows //= 2
        parts = parts[:rows] + parts[rows:]
    total = jnp.sum(jnp.sum(parts, axis=0, keepdims=True), axis=1, keepdims=True)
    flip = flip_of(total, half)
    elapsed = clock[1:2, :] + half / total
    clock[1:2, :] = elapsed
    clock[0:1, :] = jnp.where(lane_of(1) == k - 1, elapsed, clock[0:1, :])
    of_gain = jnp.zeros((HY, BZ), F32)
    of_field = jnp.zeros((HY, BZ), F32)

    def step(i, carry):
        of_gain, of_field = carry
        for j in range(UNROLL):
            x = i * UNROLL + j
            new = spin[p, x + 1, :HY] * flip(odds[x])
            spin[p, x + 1, :HY] = new
            of_gain = of_gain + new * gain[x]
            of_field = of_field + new * h[p, x]
        return of_gain, of_field

    of_gain, of_field = lax.fori_loop(0, BX // UNROLL, step, (of_gain, of_field))
    fields[p] = eighth(of_field)
    energy[k - 1] = -eighth(of_gain) - fields[1 - p]
    if halo is None:
        return
    where, x_one, x_two, y_one, y_two, z_one, z_two = halo
    one, two = far_or_near(where[1], BX + 1, 0), far_or_near(where[1], 0, BX + 1)
    spin[p, one, :HY] = spin[p, one, :HY] * flip(x_one[...])
    spin[p, two, :HY] = spin[p, two, :HY] * flip(x_two[...])
    side[p] = side[p] * flip(side_halo(where, y_one[...], y_two[...]))
    column[p] = column[p] * flip(column_halo(where, z_one[...], z_two[...]))


def rates(act, where, spin, side, column, odds, gain, h, a, v, x_one, x_two, y_one, y_two, zed, sent):
    p = 1 - act
    lane = lane_of()
    one_row = lane_of(1)
    for x in range(BX):
        first, last = spin[p, x + 1, :1], spin[p, x + 1, HY - 1 : HY]
        beyond = side[p, x : x + 1]
        spin[p, x + 1, HY + 1 : HY + 2] = roll(jnp.where(one_row < HZ, last, beyond), HZ)
        spin[p, x + 1, HY : HY + 1] = roll(jnp.where(one_row < HZ, beyond, first), HZ)
    ends = column[p]
    top = lax.broadcasted_iota(jnp.int32, (HY, BZ), 0) == 0

    def step(i, carry):
        packed, summed = carry
        for j in range(UNROLL):
            x = i * UNROLL + j
            odd = odd_row(j + act)
            here = spin[p, x + 1, :HY]
            joined = jnp.where(lane % HZ == jnp.where(odd, 0, HZ - 1), pltpu.roll(ends, (BZ + HZ - 2 * x) % BZ, 1), here)
            turned = jnp.where(odd, roll(joined, -1), roll(joined, 1))
            beside = spin[p, x, :HY] + spin[p, x + 2, :HY]
            beside = beside + jnp.where(top, spin[p, x + 1, HY + 1 : HY + 2], pltpu.roll(here, 1, 0)) + spin[p, x + 1, 1 : HY + 1]
            beside = beside + here + turned
            g = h[act, x] - 0.5 * beside
            gain[x] = g
            grown = 1.0 + jnp.exp(2.0 * spin[act, x + 1, :HY] * g)
            summed = summed + a[act, x] / grown
            root = v[x] * grown
            square = root * root
            odds[x] = square
            packed = add_face(packed, square, x, odd)
        return packed, summed

    packed, summed = lax.fori_loop(0, BX // UNROLL, step, (jnp.zeros((HY, BZ), F32), jnp.zeros((HY, BZ), F32)))
    x_one[...] = odds[far_or_near(where[1], BX - 1, 0)]
    x_two[...] = odds[far_or_near(where[1], 0, BX - 1)]
    one, two = far_or_near(where[2], HY - 1, 0), far_or_near(where[2], 0, HY - 1)
    for x in range(BX):
        y_one[x : x + 1] = odds[x, pl.ds(one, 1)]
        y_two[x : x + 1] = odds[x, pl.ds(two, 1)]
    zed[...] = packed
    sent[...] = jnp.broadcast_to(jnp.sum(summed, axis=0, keepdims=True), sent.shape)


def first_kernel(
    where, from_x_one, from_x_two, from_y_one, from_y_two, from_z_one, from_z_two, h, a, v, spin_in,
    spin, side, column, energy, fields, clock, odds, gain, x_one, x_two, y_one, y_two, zed, sent,
):
    for p in range(2):
        spin[p, far_or_near(where[1], BX + 1, 0), :HY] = from_x_one[p]
        spin[p, far_or_near(where[1], 0, BX + 1), :HY] = from_x_two[p]
        side[p] = side_halo(where, from_y_one[p], from_y_two[p])
        column[p] = column_halo(where, from_z_one[p], from_z_two[p])
    of_field = jnp.zeros((HY, BZ), F32)
    for x in range(BX):
        of_field = of_field + spin[1, x + 1, :HY] * h[1, x]
    fields[0] = jnp.zeros((8, BZ), F32)
    fields[1] = eighth(of_field)
    energy[...] = jnp.zeros(energy.shape, F32)
    clock[...] = jnp.zeros(clock.shape, F32)
    rates(0, where, spin, side, column, odds, gain, h, a, v, x_one, x_two, y_one, y_two, zed, sent)


def section_kernel(
    act, half, where, gathered, from_x_one, from_x_two, from_y_one, from_y_two, from_z_one, from_z_two, h, a, v,
    spin_in, side_in, column_in, energy_in, fields_in, clock_in, odds_in, gain_in,
    spin, side, column, energy, fields, clock, odds, gain, x_one, x_two, y_one, y_two, zed, sent,
):
    k = where[0]
    halo = (where, from_x_one, from_x_two, from_y_one, from_y_two, from_z_one, from_z_two)
    advance(k, 1 - act, half, gathered, halo, spin, side, column, odds, gain, h, energy, fields, clock)
    rates(act, where, spin, side, column, odds, gain, h, a, v, x_one, x_two, y_one, y_two, zed, sent)


def last_kernel(
    half, gathered, h, odds, gain, spin_in, energy_in, fields_in, clock_in,
    spin, energy, fields, clock, sent,
):
    advance(SECTIONS, (SECTIONS - 1) % 2, half, gathered, None, spin, None, None, odds, gain, h, energy, fields, clock)
    row = jnp.zeros((1, BZ), F32)
    for k in range(SECTIONS):
        value = jnp.sum(jnp.sum(energy[k], axis=0, keepdims=True), axis=1, keepdims=True)
        row = jnp.where(lane_of(1) == k, value, row)
    sent[...] = jnp.broadcast_to(row, sent.shape)


def unpack_kernel(spin, out):
    low = lane_of() < HZ
    narrow = shuffle_matrix(True)
    for x in range(BX):
        even_site, odd_site = spin[0, x + 1, :HY], spin[1, x + 1, :HY]
        odd = odd_row(x)
        even_z, odd_z = jnp.where(odd, odd_site, even_site), jnp.where(odd, even_site, odd_site)
        lower = jnp.where(low, even_z, roll(odd_z, HZ))
        upper = jnp.where(low, roll(even_z, HZ), odd_z)
        out[x, :HY] = matmul(lower, narrow, True)
        out[x, HY:] = matmul(upper, narrow, True)


def history_kernel(sites, gathered, clock, out):
    row = jnp.sum(gathered[...], axis=0, keepdims=True) / sites
    out[0:1, :] = row[:, :SECTIONS]
    out[1:2, :] = clock[0:1, :SECTIONS]


def call(kernel, inputs, outputs, aliases=None, far=(), far_out=(), scratch=(), flops=1000000):
    held, away = pl.BlockSpec(memory_space=pltpu.VMEM), pl.BlockSpec(memory_space=pltpu.HBM)
    inputs = [pltpu.with_memory_space_constraint(x, pltpu.HBM) if i in far else x for i, x in enumerate(inputs)]
    scalar = pl.BlockSpec(memory_space=pltpu.SMEM)
    return pl.pallas_call(
        kernel,
        out_shape=[pltpu.HBM(shape, F32) if i in far_out else jax.ShapeDtypeStruct(shape, F32) for i, shape in enumerate(outputs)],
        in_specs=[away if i in far else scalar if x.shape == (4,) else held for i, x in enumerate(inputs)],
        out_specs=[away if i in far_out else held for i in range(len(outputs))],
        input_output_aliases=aliases or {},
        scratch_shapes=scratch,
        compiler_params=pltpu.CompilerParams(vmem_limit_bytes=24 * 1024 * 1024),
        cost_estimate=pl.CostEstimate(flops=flops, bytes_accessed=1000000, transcendentals=0),
    )(*inputs)


def swap(x_one, x_two, y_one, y_two, z_one, z_two):
    got = []
    for axis, one, two in (("gx", x_one, x_two), ("gy", y_one, y_two), ("gz", z_one, z_two)):
        count = lax.axis_size(axis)
        for block, shift in ((one, 0), (two, 1)):
            pairs = [(i, (i + (1 if i % 2 == shift else -1)) % count) for i in range(count)]
            got.append(lax.ppermute(block, axis, pairs))
    return got


def spread(sent):
    return lax.all_to_all(sent, AXES, 0, 0, tiled=True)


def body(occupancy, site_field, attempt_rate, uniforms):
    devices = lax.axis_size(AXES)
    sites = float(BX * BY * BZ * devices)
    half = sites / 2.0
    tile = (HY, BZ)
    spin_shape = (2, BX + 2, PITCH, BZ)
    block = (BX, *tile)
    faces = [tile, tile, (BX, BZ), (BX, BZ), tile]
    state = [spin_shape, (2, BX, BZ), (2, *tile), (SECTIONS, 8, BZ), (2, 8, BZ), (8, BZ), block, block]
    sent_shape = (devices, BZ)
    dma = pltpu.SemaphoreType.DMA
    evens = [1 - lax.axis_index(axis) % 2 for axis in AXES]

    def where(k):
        return jnp.stack([jnp.asarray(k, jnp.int32), *evens]).astype(jnp.int32)

    spin, *sides = call(
        spins_kernel, (where(0), occupancy), [spin_shape] + [(2, *face) for face in faces], far=(1,),
        scratch=[pltpu.VMEM((BX, BY, BZ), jnp.int32), dma((BX // CHUNK,))],
    )
    halo = swap(*sides, sides[-1])
    brick = pltpu.VMEM((BX, BY, BZ), F32)
    drawn = pltpu.VMEM((BX, BY, HZ), F32)
    h, a, v = call(
        fields_kernel, (site_field, attempt_rate, uniforms), [(2, *block), (2, *block), block],
        far=(0, 1, 2), scratch=[brick, brick, drawn, dma((3,))],
    )
    carried = call(first_kernel, (where(0), *halo, h, a, v, spin), state + faces + [sent_shape], {10: 0})

    def section(k, act, carried):
        *kept, x_one, x_two, y_one, y_two, zed, sent = carried
        gathered = spread(sent)
        halo = swap(x_one, x_two, y_one, y_two, zed, zed)
        (v,) = call(
            functools.partial(draw_kernel, act), (where(k), uniforms, a), [block],
            far=(1,), scratch=[drawn, dma((1,))],
        )
        return call(
            functools.partial(section_kernel, act, half),
            (where(k), gathered, *halo, h, a, v, *kept), state + faces + [sent_shape],
            {11 + i: i for i in range(len(state))},
        )

    def pair(i, carried):
        return section(2 * i + 2, 0, section(2 * i + 1, 1, carried))

    carried = lax.fori_loop(0, SECTIONS // 2 - 1, pair, carried)
    carried = section(SECTIONS - 1, 1, carried)
    spin, _, _, energy, fields, clock, odds, gain = carried[: len(state)]
    gathered = spread(carried[-1])
    spin, energy, fields, clock, sent = call(
        functools.partial(last_kernel, half),
        (gathered, h, odds, gain, spin, energy, fields, clock),
        [spin_shape, state[3], state[4], state[5], sent_shape], {4: 0, 5: 1, 6: 2, 7: 3},
    )
    gathered = spread(sent)
    (final,) = call(unpack_kernel, (spin,), [(BX, BY, BZ)])
    (history,) = call(functools.partial(history_kernel, sites), (gathered, clock), [(2, SECTIONS)])
    return final, history


def solution(mesh):
    return jax.shard_map(
        body,
        mesh=mesh,
        in_specs=(P(*AXES), P(*AXES), P(*AXES), P(None, *AXES)),
        out_specs=(P(*AXES), P()),
        check_vma=False,
    )
```

profile of v0, /device:TPU:32, one launch (start us, length us, event | category | flops | bytes accessed | tf_op | source)
XLA Modules:
  0.0 231.5 jit_solution(10094657286362366207)
XLA Ops:
  0.7 2.7 %shard_map.59 = (f32[2,18,40,128]{3,2,1,0:T(8,128)S(1)}, f32[2,32,128]{2,1,0:T(8,128)S(1)}, f32[2,32,128]{2,1,0:T(8,128)S(1)}, f32[2,16,128]{2,1,0:T(8,128)S(1)}...) custom-call(s32[4]{0:T(128)S(1)} %add_add_fusion.3.where, s32[16,64,128]{2,1,0:T(8,128)} %occ_hbm.1), custom_call_target="tpu_custom_call" | custom-call | flops 1000000 | bytes 1000000 | tf_op jit(solution)/shard_map/pallas_call | solution.py:301
  3.6 1.6 collective-permute-start.12
  5.2 3.0 %collective-permute-start.13 = (f32[2,32,128]{2,1,0:T(8,128)S(1)}, f32[2,32,128]{2,1,0:T(8,128)S(1)}, u32[]{:S(2)}, u32[]{:S(2)}) collective-permute-start(f32[2,32,128]{2,1,0:T(8,128)S(1)} %get-tuple-element.409), channel_id=1, source_target_pairs={{0,224},{32,64},{64,32},{96,128},{128,96},{160,192},{192,160},{224... | collective-permute-start | bytes 98312 | tf_op jit(solution)/shard_map/ppermute | solution.py:319
  8.3 3.7 %collective-permute-start.17 = (f32[2,32,128]{2,1,0:T(8,128)S(1)}, f32[2,32,128]{2,1,0:T(8,128)S(1)}, u32[]{:S(2)}, u32[]{:S(2)}) collective-permute-start(f32[2,32,128]{2,1,0:T(8,128)S(1)} %get-tuple-element.412), channel_id=1, source_target_pairs={{0,7},{1,2},{2,1},{3,4},{4,3},{5,6},{6,5},{7,0},{8,15},{9,10},{10,... | collective-permute-start | bytes 98312 | tf_op jit(solution)/shard_map/ppermute | solution.py:319
  12.0 1.9 collective-permute-start.15
  13.9 2.0 shard_map.60
  16.8 2.2 shard_map.61
  19.0 146.0 %while.39 = (s32[]{:T(128)}, f32[2,18,40,128]{3,2,1,0:T(8,128)S(1)}, f32[2,16,128]{2,1,0:T(8,128)S(1)}, f32[2,32,128]{2,1,0:T(8,128)S(1)}, f32[8,8,128]{2,1,0:T(...) while((s32[]{:T(128)}, ...), condition=%wide.region_1.2_spmd, body=%wide.region_0.1_spmd.sunk | while | flops 4000029 | bytes 5442641 | solution.py:373
  19.0 10.0 %all-to-all-start = ((f32[256,1,128]{2,1,0:T(1,128)}), f32[256,1,128]{2,1,0:T(1,128)S(1)}, u32[]{:S(2)}, u32[]{:S(2)}) async-start(f32[256,1,128]{2,1,0:T(1,128)} %bitcast.38), calls=%async_computation | async-start | bytes 262144 | tf_op jit(solution)/shard_map/while/body/eval_jaxpr/all_to_all | solution.py:324
  29.2 2.0 collective-permute-start.4
  31.2 1.5 collective-permute-start.5
  32.7 1.5 collective-permute-start
  34.2 2.9 %collective-permute-start.1 = (f32[32,128]{1,0:T(8,128)S(1)}, f32[32,128]{1,0:T(8,128)S(1)}, u32[]{:S(2)}, u32[]{:S(2)}) collective-permute-start(f32[32,128]{1,0:T(8,128)S(1)} %get-tuple-element.713), channel_id=1, source_target_pairs={{0,224},{32,64},{64,32},{96,128},{128,96},{160,192},{192,160},{224... | collective-permute-start | bytes 49160 | tf_op jit(solution)/shard_map/while/body/eval_jaxpr/ppermute | solution.py:319
  37.0 1.9 collective-permute-start.3
  39.0 1.7 eval_jaxpr.12.v
  41.7 1.9 eval_jaxpr.13
  43.6 9.7 %all-to-all-start.1 = ((f32[256,1,128]{2,1,0:T(1,128)}), f32[256,1,128]{2,1,0:T(1,128)S(1)}, u32[]{:S(2)}, u32[]{:S(2)}) async-start(f32[256,1,128]{2,1,0:T(1,128)} %bitcast.40), calls=%async_computation.1 | async-start | bytes 262144 | tf_op jit(solution)/shard_map/while/body/eval_jaxpr/all_to_all | solution.py:324
  53.5 2.0 collective-permute-start.10
  57.0 1.5 collective-permute-start.6
  58.5 2.9 %collective-permute-start.7 = (f32[32,128]{1,0:T(8,128)S(1)}, f32[32,128]{1,0:T(8,128)S(1)}, u32[]{:S(2)}, u32[]{:S(2)}) collective-permute-start(f32[32,128]{1,0:T(8,128)S(1)} %get-tuple-element.654), channel_id=1, source_target_pairs={{0,224},{32,64},{64,32},{96,128},{128,96},{160,192},{192,160},{224... | collective-permute-start | bytes 49160 | tf_op jit(solution)/shard_map/while/body/eval_jaxpr/ppermute | solution.py:319
  61.3 1.9 collective-permute-start.9
  63.3 1.7 eval_jaxpr.14.v
  66.0 1.9 eval_jaxpr.15
  67.9 9.7 %all-to-all-start = ((f32[256,1,128]{2,1,0:T(1,128)}), f32[256,1,128]{2,1,0:T(1,128)S(1)}, u32[]{:S(2)}, u32[]{:S(2)}) async-start(f32[256,1,128]{2,1,0:T(1,128)} %bitcast.38), calls=%async_computation | async-start | bytes 262144 | tf_op jit(solution)/shard_map/while/body/eval_jaxpr/all_to_all | solution.py:324
  77.8 2.0 collective-permute-start.4
  79.8 1.5 collective-permute-start.5
  81.2 1.5 collective-permute-start
  82.7 2.9 %collective-permute-start.1 = (f32[32,128]{1,0:T(8,128)S(1)}, f32[32,128]{1,0:T(8,128)S(1)}, u32[]{:S(2)}, u32[]{:S(2)}) collective-permute-start(f32[32,128]{1,0:T(8,128)S(1)} %get-tuple-element.713), channel_id=1, source_target_pairs={{0,224},{32,64},{64,32},{96,128},{128,96},{160,192},{192,160},{224... | collective-permute-start | bytes 49160 | tf_op jit(solution)/shard_map/while/body/eval_jaxpr/ppermute | solution.py:319
  85.6 1.9 collective-permute-start.3
  87.5 1.7 eval_jaxpr.12.v
  90.2 1.9 eval_jaxpr.13
  92.1 9.7 %all-to-all-start.1 = ((f32[256,1,128]{2,1,0:T(1,128)}), f32[256,1,128]{2,1,0:T(1,128)S(1)}, u32[]{:S(2)}, u32[]{:S(2)}) async-start(f32[256,1,128]{2,1,0:T(1,128)} %bitcast.40), calls=%async_computation.1 | async-start | bytes 262144 | tf_op jit(solution)/shard_map/while/body/eval_jaxpr/all_to_all | solution.py:324
  102.1 2.0 collective-permute-start.10
  105.5 1.5 collective-permute-start.6
  107.0 2.9 %collective-permute-start.7 = (f32[32,128]{1,0:T(8,128)S(1)}, f32[32,128]{1,0:T(8,128)S(1)}, u32[]{:S(2)}, u32[]{:S(2)}) collective-permute-start(f32[32,128]{1,0:T(8,128)S(1)} %get-tuple-element.654), channel_id=1, source_target_pairs={{0,224},{32,64},{64,32},{96,128},{128,96},{160,192},{192,160},{224... | collective-permute-start | bytes 49160 | tf_op jit(solution)/shard_map/while/body/eval_jaxpr/ppermute | solution.py:319
  109.9 1.9 collective-permute-start.9
  111.8 1.7 eval_jaxpr.14.v
  114.5 1.9 eval_jaxpr.15
  116.4 9.7 %all-to-all-start = ((f32[256,1,128]{2,1,0:T(1,128)}), f32[256,1,128]{2,1,0:T(1,128)S(1)}, u32[]{:S(2)}, u32[]{:S(2)}) async-start(f32[256,1,128]{2,1,0:T(1,128)} %bitcast.38), calls=%async_computation | async-start | bytes 262144 | tf_op jit(solution)/shard_map/while/body/eval_jaxpr/all_to_all | solution.py:324
  126.3 2.0 collective-permute-start.4
  128.3 1.5 collective-permute-start.5
  129.8 1.5 collective-permute-start
  131.3 2.9 %collective-permute-start.1 = (f32[32,128]{1,0:T(8,128)S(1)}, f32[32,128]{1,0:T(8,128)S(1)}, u32[]{:S(2)}, u32[]{:S(2)}) collective-permute-start(f32[32,128]{1,0:T(8,128)S(1)} %get-tuple-element.713), channel_id=1, source_target_pairs={{0,224},{32,64},{64,32},{96,128},{128,96},{160,192},{192,160},{224... | collective-permute-start | bytes 49160 | tf_op jit(solution)/shard_map/while/body/eval_jaxpr/ppermute | solution.py:319
  134.1 1.9 collective-permute-start.3
  136.1 1.7 eval_jaxpr.12.v
  138.8 1.9 eval_jaxpr.13
  140.7 9.7 %all-to-all-start.1 = ((f32[256,1,128]{2,1,0:T(1,128)}), f32[256,1,128]{2,1,0:T(1,128)S(1)}, u32[]{:S(2)}, u32[]{:S(2)}) async-start(f32[256,1,128]{2,1,0:T(1,128)} %bitcast.40), calls=%async_computation.1 | async-start | bytes 262144 | tf_op jit(solution)/shard_map/while/body/eval_jaxpr/all_to_all | solution.py:324
  150.6 2.0 collective-permute-start.10
  154.1 1.5 collective-permute-start.6
  155.5 2.9 %collective-permute-start.7 = (f32[32,128]{1,0:T(8,128)S(1)}, f32[32,128]{1,0:T(8,128)S(1)}, u32[]{:S(2)}, u32[]{:S(2)}) collective-permute-start(f32[32,128]{1,0:T(8,128)S(1)} %get-tuple-element.654), channel_id=1, source_target_pairs={{0,224},{32,64},{64,32},{96,128},{128,96},{160,192},{192,160},{224... | collective-permute-start | bytes 49160 | tf_op jit(solution)/shard_map/while/body/eval_jaxpr/ppermute | solution.py:319
  158.4 1.9 collective-permute-start.9
  160.3 1.7 eval_jaxpr.14.v
  163.1 1.9 eval_jaxpr.15
  165.0 9.7 %all-to-all-start.2 = ((f32[256,1,128]{2,1,0:T(1,128)}), f32[256,1,128]{2,1,0:T(1,128)S(1)}, u32[]{:S(2)}, u32[]{:S(2)}) async-start(f32[256,1,128]{2,1,0:T(1,128)} %bitcast.14), calls=%async_computation.2 | async-start | bytes 262144 | tf_op jit(solution)/shard_map/all_to_all | solution.py:324
  174.9 2.0 collective-permute-start.22
  178.3 1.5 collective-permute-start.18
  179.8 2.9 %collective-permute-start.19 = (f32[32,128]{1,0:T(8,128)S(1)}, f32[32,128]{1,0:T(8,128)S(1)}, u32[]{:S(2)}, u32[]{:S(2)}) collective-permute-start(f32[32,128]{1,0:T(8,128)S(1)} %get-tuple-element.433), channel_id=1, source_target_pairs={{0,224},{32,64},{64,32},{96,128},{128,96},{160,192},{192,160},{224... | collective-permute-start | bytes 49160 | tf_op jit(solution)/shard_map/ppermute | solution.py:319
  182.7 1.9 collective-permute-start.21
  184.6 1.7 shard_map.62.v
  187.3 1.9 shard_map.63
  189.2 22.1 %all_to_all.53 = f32[256,1,128]{2,1,0:T(1,128)S(1)} all-to-all(f32[256,1,128]{2,1,0:T(1,128)S(1)} %bitcast.47), channel_id=1, replica_groups=mesh['gx'=8,'gy'=4,'gz'=8] {'gx','gy','gz'}, dimensions={0} | all-to-all | bytes 262144 | tf_op jit(solution)/shard_map/all_to_all | solution.py:324
  212.2 6.1 %all-to-all-start.4 = ((f32[256,1,128]{2,1,0:T(1,128)}), f32[256,1,128]{2,1,0:T(1,128)S(1)}, u32[]{:S(2)}, u32[]{:S(2)}) async-start(f32[256,1,128]{2,1,0:T(1,128)} %bitcast.20), calls=%async_computation.4 | async-start | bytes 262144 | tf_op jit(solution)/shard_map/all_to_all | solution.py:324
  218.3 2.6 %shard_map.65 = f32[16,64,128]{2,1,0:T(8,128)} custom-call(f32[2,18,40,128]{3,2,1,0:T(8,128)S(1)} %get-tuple-element.452.spin), custom_call_target="tpu_custom_call" | custom-call | flops 1000000 | bytes 1000000 | tf_op jit(solution)/shard_map/pallas_call | solution.py:301
  220.9 10.0 %all-to-all-done.4 = f32[256,1,128]{2,1,0:T(1,128)S(1)} async-done(((f32[256,1,128]{2,1,0:T(1,128)}), f32[256,1,128]{2,1,0:T(1,128)S(1)}, u32[]{:S(2)}, u32[]{:S(2)}) %all-to-all-start.4) | async-done | bytes 131104 | tf_op jit(solution)/shard_map/all_to_all | solution.py:324
  (78 shorter events, 17.1 us)
Async XLA Ops:
  3.5 8.5 %collective-permute-start.14 = (f32[2,16,128]{2,1,0:T(8,128)S(1)}, f32[2,16,128]{2,1,0:T(8,128)S(1)}, u32[]{:S(2)}, u32[]{:S(2)}) collective-permute-start(f32[2,16,128]{2,1,0:T(8,128)S(1)} %get-tuple-element.410), channel_id=1, source_target_pairs={{0,8},{8,0},{16,24},{24,16},{1,9},{9,1},{17,25},{25,17},{2,10},{10... | collective-permute-start | bytes 49160 | tf_op jit(solution)/shard_map/ppermute | solution.py:319
  3.6 13.2 %collective-permute-start.12 = (f32[2,32,128]{2,1,0:T(8,128)S(1)}, f32[2,32,128]{2,1,0:T(8,128)S(1)}, u32[]{:S(2)}, u32[]{:S(2)}) collective-permute-start(f32[2,32,128]{2,1,0:T(8,128)S(1)} %get-tuple-element.408), channel_id=1, source_target_pairs={{0,32},{32,0},{64,96},{96,64},{128,160},{160,128},{192,224},{224,1... | collective-permute-start | bytes 98312 | tf_op jit(solution)/shard_map/ppermute | solution.py:319
  5.2 11.6 %collective-permute-start.13 = (f32[2,32,128]{2,1,0:T(8,128)S(1)}, f32[2,32,128]{2,1,0:T(8,128)S(1)}, u32[]{:S(2)}, u32[]{:S(2)}) collective-permute-start(f32[2,32,128]{2,1,0:T(8,128)S(1)} %get-tuple-element.409), channel_id=1, source_target_pairs={{0,224},{32,64},{64,32},{96,128},{128,96},{160,192},{192,160},{224... | collective-permute-start | bytes 98312 | tf_op jit(solution)/shard_map/ppermute | solution.py:319
  8.2 8.6 %collective-permute-start.16 = (f32[2,32,128]{2,1,0:T(8,128)S(1)}, f32[2,32,128]{2,1,0:T(8,128)S(1)}, u32[]{:S(2)}, u32[]{:S(2)}) collective-permute-start(f32[2,32,128]{2,1,0:T(8,128)S(1)} %get-tuple-element.412), channel_id=1, source_target_pairs={{0,1},{1,0},{2,3},{3,2},{4,5},{5,4},{6,7},{7,6},{8,9},{9,8},{10,11... | collective-permute-start | bytes 98312 | tf_op jit(solution)/shard_map/ppermute | solution.py:319
  8.3 8.5 %collective-permute-start.17 = (f32[2,32,128]{2,1,0:T(8,128)S(1)}, f32[2,32,128]{2,1,0:T(8,128)S(1)}, u32[]{:S(2)}, u32[]{:S(2)}) collective-permute-start(f32[2,32,128]{2,1,0:T(8,128)S(1)} %get-tuple-element.412), channel_id=1, source_target_pairs={{0,7},{1,2},{2,1},{3,4},{4,3},{5,6},{6,5},{7,0},{8,15},{9,10},{10,... | collective-permute-start | bytes 98312 | tf_op jit(solution)/shard_map/ppermute | solution.py:319
  12.0 4.8 %collective-permute-start.15 = (f32[2,16,128]{2,1,0:T(8,128)S(1)}, f32[2,16,128]{2,1,0:T(8,128)S(1)}, u32[]{:S(2)}, u32[]{:S(2)}) collective-permute-start(f32[2,16,128]{2,1,0:T(8,128)S(1)} %get-tuple-element.411), channel_id=1, source_target_pairs={{0,24},{8,16},{16,8},{24,0},{1,25},{9,17},{17,9},{25,1},{2,26},{10... | collective-permute-start | bytes 49160 | tf_op jit(solution)/shard_map/ppermute | solution.py:319
  19.0 22.7 %all-to-all-start = ((f32[256,1,128]{2,1,0:T(1,128)}), f32[256,1,128]{2,1,0:T(1,128)S(1)}, u32[]{:S(2)}, u32[]{:S(2)}) async-start(f32[256,1,128]{2,1,0:T(1,128)} %bitcast.38), calls=%async_computation | async-start | bytes 262144 | tf_op jit(solution)/shard_map/while/body/eval_jaxpr/all_to_all | solution.py:324
  29.0 8.0 %collective-permute-start.2 = (f32[16,128]{1,0:T(8,128)S(1)}, f32[16,128]{1,0:T(8,128)S(1)}, u32[]{:S(2)}, u32[]{:S(2)}) collective-permute-start(f32[16,128]{1,0:T(8,128)S(1)} %get-tuple-element.714), channel_id=1, source_target_pairs={{0,8},{8,0},{16,24},{24,16},{1,9},{9,1},{17,25},{25,17},{2,10},{10... | collective-permute-start | bytes 24584 | tf_op jit(solution)/shard_map/while/body/eval_jaxpr/ppermute | solution.py:319
  29.2 12.4 %collective-permute-start.4 = (f32[32,128]{1,0:T(8,128)S(1)}, f32[32,128]{1,0:T(8,128)S(1)}, u32[]{:S(2)}, u32[]{:S(2)}) collective-permute-start(f32[32,128]{1,0:T(8,128)S(1)} %get-tuple-element.716), channel_id=1, source_target_pairs={{0,1},{1,0},{2,3},{3,2},{4,5},{5,4},{6,7},{7,6},{8,9},{9,8},{10,11... | collective-permute-start | bytes 49160 | tf_op jit(solution)/shard_map/while/body/eval_jaxpr/ppermute | solution.py:319
  31.2 10.4 %collective-permute-start.5 = (f32[32,128]{1,0:T(8,128)S(1)}, f32[32,128]{1,0:T(8,128)S(1)}, u32[]{:S(2)}, u32[]{:S(2)}) collective-permute-start(f32[32,128]{1,0:T(8,128)S(1)} %get-tuple-element.716), channel_id=1, source_target_pairs={{0,7},{1,2},{2,1},{3,4},{4,3},{5,6},{6,5},{7,0},{8,15},{9,10},{10,... | collective-permute-start | bytes 49160 | tf_op jit(solution)/shard_map/while/body/eval_jaxpr/ppermute | solution.py:319
  32.7 9.0 %collective-permute-start = (f32[32,128]{1,0:T(8,128)S(1)}, f32[32,128]{1,0:T(8,128)S(1)}, u32[]{:S(2)}, u32[]{:S(2)}) collective-permute-start(f32[32,128]{1,0:T(8,128)S(1)} %get-tuple-element.712), channel_id=1, source_target_pairs={{0,32},{32,0},{64,96},{96,64},{128,160},{160,128},{192,224},{224,1... | collective-permute-start | bytes 49160 | tf_op jit(solution)/shard_map/while/body/eval_jaxpr/ppermute | solution.py:319
  34.2 7.5 %collective-permute-start.1 = (f32[32,128]{1,0:T(8,128)S(1)}, f32[32,128]{1,0:T(8,128)S(1)}, u32[]{:S(2)}, u32[]{:S(2)}) collective-permute-start(f32[32,128]{1,0:T(8,128)S(1)} %get-tuple-element.713), channel_id=1, source_target_pairs={{0,224},{32,64},{64,32},{96,128},{128,96},{160,192},{192,160},{224... | collective-permute-start | bytes 49160 | tf_op jit(solution)/shard_map/while/body/eval_jaxpr/ppermute | solution.py:319
  37.0 4.6 %collective-permute-start.3 = (f32[16,128]{1,0:T(8,128)S(1)}, f32[16,128]{1,0:T(8,128)S(1)}, u32[]{:S(2)}, u32[]{:S(2)}) collective-permute-start(f32[16,128]{1,0:T(8,128)S(1)} %get-tuple-element.715), channel_id=1, source_target_pairs={{0,24},{8,16},{16,8},{24,0},{1,25},{9,17},{17,9},{25,1},{2,26},{10... | collective-permute-start | bytes 24584 | tf_op jit(solution)/shard_map/while/body/eval_jaxpr/ppermute | solution.py:319
  43.6 22.4 %all-to-all-start.1 = ((f32[256,1,128]{2,1,0:T(1,128)}), f32[256,1,128]{2,1,0:T(1,128)S(1)}, u32[]{:S(2)}, u32[]{:S(2)}) async-start(f32[256,1,128]{2,1,0:T(1,128)} %bitcast.40), calls=%async_computation.1 | async-start | bytes 262144 | tf_op jit(solution)/shard_map/while/body/eval_jaxpr/all_to_all | solution.py:324
  53.3 8.0 %collective-permute-start.8 = (f32[16,128]{1,0:T(8,128)S(1)}, f32[16,128]{1,0:T(8,128)S(1)}, u32[]{:S(2)}, u32[]{:S(2)}) collective-permute-start(f32[16,128]{1,0:T(8,128)S(1)} %get-tuple-element.655), channel_id=1, source_target_pairs={{0,8},{8,0},{16,24},{24,16},{1,9},{9,1},{17,25},{25,17},{2,10},{10... | collective-permute-start | bytes 24584 | tf_op jit(solution)/shard_map/while/body/eval_jaxpr/ppermute | solution.py:319
  53.5 12.4 %collective-permute-start.10 = (f32[32,128]{1,0:T(8,128)S(1)}, f32[32,128]{1,0:T(8,128)S(1)}, u32[]{:S(2)}, u32[]{:S(2)}) collective-permute-start(f32[32,128]{1,0:T(8,128)S(1)} %get-tuple-element.657), channel_id=1, source_target_pairs={{0,1},{1,0},{2,3},{3,2},{4,5},{5,4},{6,7},{7,6},{8,9},{9,8},{10,11... | collective-permute-start | bytes 49160 | tf_op jit(solution)/shard_map/while/body/eval_jaxpr/ppermute | solution.py:319
  55.5 10.4 %collective-permute-start.11 = (f32[32,128]{1,0:T(8,128)S(1)}, f32[32,128]{1,0:T(8,128)S(1)}, u32[]{:S(2)}, u32[]{:S(2)}) collective-permute-start(f32[32,128]{1,0:T(8,128)S(1)} %get-tuple-element.657), channel_id=1, source_target_pairs={{0,7},{1,2},{2,1},{3,4},{4,3},{5,6},{6,5},{7,0},{8,15},{9,10},{10,... | collective-permute-start | bytes 49160 | tf_op jit(solution)/shard_map/while/body/eval_jaxpr/ppermute | solution.py:319
  57.0 9.0 %collective-permute-start.6 = (f32[32,128]{1,0:T(8,128)S(1)}, f32[32,128]{1,0:T(8,128)S(1)}, u32[]{:S(2)}, u32[]{:S(2)}) collective-permute-start(f32[32,128]{1,0:T(8,128)S(1)} %get-tuple-element.653), channel_id=1, source_target_pairs={{0,32},{32,0},{64,96},{96,64},{128,160},{160,128},{192,224},{224,1... | collective-permute-start | bytes 49160 | tf_op jit(solution)/shard_map/while/body/eval_jaxpr/ppermute | solution.py:319
  58.5 7.5 %collective-permute-start.7 = (f32[32,128]{1,0:T(8,128)S(1)}, f32[32,128]{1,0:T(8,128)S(1)}, u32[]{:S(2)}, u32[]{:S(2)}) collective-permute-start(f32[32,128]{1,0:T(8,128)S(1)} %get-tuple-element.654), channel_id=1, source_target_pairs={{0,224},{32,64},{64,32},{96,128},{128,96},{160,192},{192,160},{224... | collective-permute-start | bytes 49160 | tf_op jit(solution)/shard_map/while/body/eval_jaxpr/ppermute | solution.py:319
  61.3 4.6 %collective-permute-start.9 = (f32[16,128]{1,0:T(8,128)S(1)}, f32[16,128]{1,0:T(8,128)S(1)}, u32[]{:S(2)}, u32[]{:S(2)}) collective-permute-start(f32[16,128]{1,0:T(8,128)S(1)} %get-tuple-element.656), channel_id=1, source_target_pairs={{0,24},{8,16},{16,8},{24,0},{1,25},{9,17},{17,9},{25,1},{2,26},{10... | collective-permute-start | bytes 24584 | tf_op jit(solution)/shard_map/while/body/eval_jaxpr/ppermute | solution.py:319
  67.9 22.4 %all-to-all-start = ((f32[256,1,128]{2,1,0:T(1,128)}), f32[256,1,128]{2,1,0:T(1,128)S(1)}, u32[]{:S(2)}, u32[]{:S(2)}) async-start(f32[256,1,128]{2,1,0:T(1,128)} %bitcast.38), calls=%async_computation | async-start | bytes 262144 | tf_op jit(solution)/shard_map/while/body/eval_jaxpr/all_to_all | solution.py:324
  77.6 8.0 %collective-permute-start.2 = (f32[16,128]{1,0:T(8,128)S(1)}, f32[16,128]{1,0:T(8,128)S(1)}, u32[]{:S(2)}, u32[]{:S(2)}) collective-permute-start(f32[16,128]{1,0:T(8,128)S(1)} %get-tuple-element.714), channel_id=1, source_target_pairs={{0,8},{8,0},{16,24},{24,16},{1,9},{9,1},{17,25},{25,17},{2,10},{10... | collective-permute-start | bytes 24584 | tf_op jit(solution)/shard_map/while/body/eval_jaxpr/ppermute | solution.py:319
  77.8 12.4 %collective-permute-start.4 = (f32[32,128]{1,0:T(8,128)S(1)}, f32[32,128]{1,0:T(8,128)S(1)}, u32[]{:S(2)}, u32[]{:S(2)}) collective-permute-start(f32[32,128]{1,0:T(8,128)S(1)} %get-tuple-element.716), channel_id=1, source_target_pairs={{0,1},{1,0},{2,3},{3,2},{4,5},{5,4},{6,7},{7,6},{8,9},{9,8},{10,11... | collective-permute-start | bytes 49160 | tf_op jit(solution)/shard_map/while/body/eval_jaxpr/ppermute | solution.py:319
  79.8 10.4 %collective-permute-start.5 = (f32[32,128]{1,0:T(8,128)S(1)}, f32[32,128]{1,0:T(8,128)S(1)}, u32[]{:S(2)}, u32[]{:S(2)}) collective-permute-start(f32[32,128]{1,0:T(8,128)S(1)} %get-tuple-element.716), channel_id=1, source_target_pairs={{0,7},{1,2},{2,1},{3,4},{4,3},{5,6},{6,5},{7,0},{8,15},{9,10},{10,... | collective-permute-start | bytes 49160 | tf_op jit(solution)/shard_map/while/body/eval_jaxpr/ppermute | solution.py:319
  81.2 9.0 %collective-permute-start = (f32[32,128]{1,0:T(8,128)S(1)}, f32[32,128]{1,0:T(8,128)S(1)}, u32[]{:S(2)}, u32[]{:S(2)}) collective-permute-start(f32[32,128]{1,0:T(8,128)S(1)} %get-tuple-element.712), channel_id=1, source_target_pairs={{0,32},{32,0},{64,96},{96,64},{128,160},{160,128},{192,224},{224,1... | collective-permute-start | bytes 49160 | tf_op jit(solution)/shard_map/while/body/eval_jaxpr/ppermute | solution.py:319
  82.7 7.5 %collective-permute-start.1 = (f32[32,128]{1,0:T(8,128)S(1)}, f32[32,128]{1,0:T(8,128)S(1)}, u32[]{:S(2)}, u32[]{:S(2)}) collective-permute-start(f32[32,128]{1,0:T(8,128)S(1)} %get-tuple-element.713), channel_id=1, source_target_pairs={{0,224},{32,64},{64,32},{96,128},{128,96},{160,192},{192,160},{224... | collective-permute-start | bytes 49160 | tf_op jit(solution)/shard_map/while/body/eval_jaxpr/ppermute | solution.py:319
  85.6 4.6 %collective-permute-start.3 = (f32[16,128]{1,0:T(8,128)S(1)}, f32[16,128]{1,0:T(8,128)S(1)}, u32[]{:S(2)}, u32[]{:S(2)}) collective-permute-start(f32[16,128]{1,0:T(8,128)S(1)} %get-tuple-element.715), channel_id=1, source_target_pairs={{0,24},{8,16},{16,8},{24,0},{1,25},{9,17},{17,9},{25,1},{2,26},{10... | collective-permute-start | bytes 24584 | tf_op jit(solution)/shard_map/while/body/eval_jaxpr/ppermute | solution.py:319
  92.1 22.4 %all-to-all-start.1 = ((f32[256,1,128]{2,1,0:T(1,128)}), f32[256,1,128]{2,1,0:T(1,128)S(1)}, u32[]{:S(2)}, u32[]{:S(2)}) async-start(f32[256,1,128]{2,1,0:T(1,128)} %bitcast.40), calls=%async_computation.1 | async-start | bytes 262144 | tf_op jit(solution)/shard_map/while/body/eval_jaxpr/all_to_all | solution.py:324
  101.8 8.0 %collective-permute-start.8 = (f32[16,128]{1,0:T(8,128)S(1)}, f32[16,128]{1,0:T(8,128)S(1)}, u32[]{:S(2)}, u32[]{:S(2)}) collective-permute-start(f32[16,128]{1,0:T(8,128)S(1)} %get-tuple-element.655), channel_id=1, source_target_pairs={{0,8},{8,0},{16,24},{24,16},{1,9},{9,1},{17,25},{25,17},{2,10},{10... | collective-permute-start | bytes 24584 | tf_op jit(solution)/shard_map/while/body/eval_jaxpr/ppermute | solution.py:319
  102.1 12.4 %collective-permute-start.10 = (f32[32,128]{1,0:T(8,128)S(1)}, f32[32,128]{1,0:T(8,128)S(1)}, u32[]{:S(2)}, u32[]{:S(2)}) collective-permute-start(f32[32,128]{1,0:T(8,128)S(1)} %get-tuple-element.657), channel_id=1, source_target_pairs={{0,1},{1,0},{2,3},{3,2},{4,5},{5,4},{6,7},{7,6},{8,9},{9,8},{10,11... | collective-permute-start | bytes 49160 | tf_op jit(solution)/shard_map/while/body/eval_jaxpr/ppermute | solution.py:319
  104.1 10.4 %collective-permute-start.11 = (f32[32,128]{1,0:T(8,128)S(1)}, f32[32,128]{1,0:T(8,128)S(1)}, u32[]{:S(2)}, u32[]{:S(2)}) collective-permute-start(f32[32,128]{1,0:T(8,128)S(1)} %get-tuple-element.657), channel_id=1, source_target_pairs={{0,7},{1,2},{2,1},{3,4},{4,3},{5,6},{6,5},{7,0},{8,15},{9,10},{10,... | collective-permute-start | bytes 49160 | tf_op jit(solution)/shard_map/while/body/eval_jaxpr/ppermute | solution.py:319
  105.5 9.0 %collective-permute-start.6 = (f32[32,128]{1,0:T(8,128)S(1)}, f32[32,128]{1,0:T(8,128)S(1)}, u32[]{:S(2)}, u32[]{:S(2)}) collective-permute-start(f32[32,128]{1,0:T(8,128)S(1)} %get-tuple-element.653), channel_id=1, source_target_pairs={{0,32},{32,0},{64,96},{96,64},{128,160},{160,128},{192,224},{224,1... | collective-permute-start | bytes 49160 | tf_op jit(solution)/shard_map/while/body/eval_jaxpr/ppermute | solution.py:319
  107.0 7.5 %collective-permute-start.7 = (f32[32,128]{1,0:T(8,128)S(1)}, f32[32,128]{1,0:T(8,128)S(1)}, u32[]{:S(2)}, u32[]{:S(2)}) collective-permute-start(f32[32,128]{1,0:T(8,128)S(1)} %get-tuple-element.654), channel_id=1, source_target_pairs={{0,224},{32,64},{64,32},{96,128},{128,96},{160,192},{192,160},{224... | collective-permute-start | bytes 49160 | tf_op jit(solution)/shard_map/while/body/eval_jaxpr/ppermute | solution.py:319
  109.9 4.6 %collective-permute-start.9 = (f32[16,128]{1,0:T(8,128)S(1)}, f32[16,128]{1,0:T(8,128)S(1)}, u32[]{:S(2)}, u32[]{:S(2)}) collective-permute-start(f32[16,128]{1,0:T(8,128)S(1)} %get-tuple-element.656), channel_id=1, source_target_pairs={{0,24},{8,16},{16,8},{24,0},{1,25},{9,17},{17,9},{25,1},{2,26},{10... | collective-permute-start | bytes 24584 | tf_op jit(solution)/shard_map/while/body/eval_jaxpr/ppermute | solution.py:319
  116.4 22.4 %all-to-all-start = ((f32[256,1,128]{2,1,0:T(1,128)}), f32[256,1,128]{2,1,0:T(1,128)S(1)}, u32[]{:S(2)}, u32[]{:S(2)}) async-start(f32[256,1,128]{2,1,0:T(1,128)} %bitcast.38), calls=%async_computation | async-start | bytes 262144 | tf_op jit(solution)/shard_map/while/body/eval_jaxpr/all_to_all | solution.py:324
  126.1 8.0 %collective-permute-start.2 = (f32[16,128]{1,0:T(8,128)S(1)}, f32[16,128]{1,0:T(8,128)S(1)}, u32[]{:S(2)}, u32[]{:S(2)}) collective-permute-start(f32[16,128]{1,0:T(8,128)S(1)} %get-tuple-element.714), channel_id=1, source_target_pairs={{0,8},{8,0},{16,24},{24,16},{1,9},{9,1},{17,25},{25,17},{2,10},{10... | collective-permute-start | bytes 24584 | tf_op jit(solution)/shard_map/while/body/eval_jaxpr/ppermute | solution.py:319
  126.3 12.4 %collective-permute-start.4 = (f32[32,128]{1,0:T(8,128)S(1)}, f32[32,128]{1,0:T(8,128)S(1)}, u32[]{:S(2)}, u32[]{:S(2)}) collective-permute-start(f32[32,128]{1,0:T(8,128)S(1)} %get-tuple-element.716), channel_id=1, source_target_pairs={{0,1},{1,0},{2,3},{3,2},{4,5},{5,4},{6,7},{7,6},{8,9},{9,8},{10,11... | collective-permute-start | bytes 49160 | tf_op jit(solution)/shard_map/while/body/eval_jaxpr/ppermute | solution.py:319
  128.3 10.4 %collective-permute-start.5 = (f32[32,128]{1,0:T(8,128)S(1)}, f32[32,128]{1,0:T(8,128)S(1)}, u32[]{:S(2)}, u32[]{:S(2)}) collective-permute-start(f32[32,128]{1,0:T(8,128)S(1)} %get-tuple-element.716), channel_id=1, source_target_pairs={{0,7},{1,2},{2,1},{3,4},{4,3},{5,6},{6,5},{7,0},{8,15},{9,10},{10,... | collective-permute-start | bytes 49160 | tf_op jit(solution)/shard_map/while/body/eval_jaxpr/ppermute | solution.py:319
  129.8 9.0 %collective-permute-start = (f32[32,128]{1,0:T(8,128)S(1)}, f32[32,128]{1,0:T(8,128)S(1)}, u32[]{:S(2)}, u32[]{:S(2)}) collective-permute-start(f32[32,128]{1,0:T(8,128)S(1)} %get-tuple-element.712), channel_id=1, source_target_pairs={{0,32},{32,0},{64,96},{96,64},{128,160},{160,128},{192,224},{224,1... | collective-permute-start | bytes 49160 | tf_op jit(solution)/shard_map/while/body/eval_jaxpr/ppermute | solution.py:319
  131.3 7.5 %collective-permute-start.1 = (f32[32,128]{1,0:T(8,128)S(1)}, f32[32,128]{1,0:T(8,128)S(1)}, u32[]{:S(2)}, u32[]{:S(2)}) collective-permute-start(f32[32,128]{1,0:T(8,128)S(1)} %get-tuple-element.713), channel_id=1, source_target_pairs={{0,224},{32,64},{64,32},{96,128},{128,96},{160,192},{192,160},{224... | collective-permute-start | bytes 49160 | tf_op jit(solution)/shard_map/while/body/eval_jaxpr/ppermute | solution.py:319
  134.1 4.6 %collective-permute-start.3 = (f32[16,128]{1,0:T(8,128)S(1)}, f32[16,128]{1,0:T(8,128)S(1)}, u32[]{:S(2)}, u32[]{:S(2)}) collective-permute-start(f32[16,128]{1,0:T(8,128)S(1)} %get-tuple-element.715), channel_id=1, source_target_pairs={{0,24},{8,16},{16,8},{24,0},{1,25},{9,17},{17,9},{25,1},{2,26},{10... | collective-permute-start | bytes 24584 | tf_op jit(solution)/shard_map/while/body/eval_jaxpr/ppermute | solution.py:319
  140.7 22.4 %all-to-all-start.1 = ((f32[256,1,128]{2,1,0:T(1,128)}), f32[256,1,128]{2,1,0:T(1,128)S(1)}, u32[]{:S(2)}, u32[]{:S(2)}) async-start(f32[256,1,128]{2,1,0:T(1,128)} %bitcast.40), calls=%async_computation.1 | async-start | bytes 262144 | tf_op jit(solution)/shard_map/while/body/eval_jaxpr/all_to_all | solution.py:324
  150.4 8.0 %collective-permute-start.8 = (f32[16,128]{1,0:T(8,128)S(1)}, f32[16,128]{1,0:T(8,128)S(1)}, u32[]{:S(2)}, u32[]{:S(2)}) collective-permute-start(f32[16,128]{1,0:T(8,128)S(1)} %get-tuple-element.655), channel_id=1, source_target_pairs={{0,8},{8,0},{16,24},{24,16},{1,9},{9,1},{17,25},{25,17},{2,10},{10... | collective-permute-start | bytes 24584 | tf_op jit(solution)/shard_map/while/body/eval_jaxpr/ppermute | solution.py:319
  150.6 12.4 %collective-permute-start.10 = (f32[32,128]{1,0:T(8,128)S(1)}, f32[32,128]{1,0:T(8,128)S(1)}, u32[]{:S(2)}, u32[]{:S(2)}) collective-permute-start(f32[32,128]{1,0:T(8,128)S(1)} %get-tuple-element.657), channel_id=1, source_target_pairs={{0,1},{1,0},{2,3},{3,2},{4,5},{5,4},{6,7},{7,6},{8,9},{9,8},{10,11... | collective-permute-start | bytes 49160 | tf_op jit(solution)/shard_map/while/body/eval_jaxpr/ppermute | solution.py:319
  152.6 10.4 %collective-permute-start.11 = (f32[32,128]{1,0:T(8,128)S(1)}, f32[32,128]{1,0:T(8,128)S(1)}, u32[]{:S(2)}, u32[]{:S(2)}) collective-permute-start(f32[32,128]{1,0:T(8,128)S(1)} %get-tuple-element.657), channel_id=1, source_target_pairs={{0,7},{1,2},{2,1},{3,4},{4,3},{5,6},{6,5},{7,0},{8,15},{9,10},{10,... | collective-permute-start | bytes 49160 | tf_op jit(solution)/shard_map/while/body/eval_jaxpr/ppermute | solution.py:319
  154.1 9.0 %collective-permute-start.6 = (f32[32,128]{1,0:T(8,128)S(1)}, f32[32,128]{1,0:T(8,128)S(1)}, u32[]{:S(2)}, u32[]{:S(2)}) collective-permute-start(f32[32,128]{1,0:T(8,128)S(1)} %get-tuple-element.653), channel_id=1, source_target_pairs={{0,32},{32,0},{64,96},{96,64},{128,160},{160,128},{192,224},{224,1... | collective-permute-start | bytes 49160 | tf_op jit(solution)/shard_map/while/body/eval_jaxpr/ppermute | solution.py:319
  155.5 7.5 %collective-permute-start.7 = (f32[32,128]{1,0:T(8,128)S(1)}, f32[32,128]{1,0:T(8,128)S(1)}, u32[]{:S(2)}, u32[]{:S(2)}) collective-permute-start(f32[32,128]{1,0:T(8,128)S(1)} %get-tuple-element.654), channel_id=1, source_target_pairs={{0,224},{32,64},{64,32},{96,128},{128,96},{160,192},{192,160},{224... | collective-permute-start | bytes 49160 | tf_op jit(solution)/shard_map/while/body/eval_jaxpr/ppermute | solution.py:319
  158.4 4.6 %collective-permute-start.9 = (f32[16,128]{1,0:T(8,128)S(1)}, f32[16,128]{1,0:T(8,128)S(1)}, u32[]{:S(2)}, u32[]{:S(2)}) collective-permute-start(f32[16,128]{1,0:T(8,128)S(1)} %get-tuple-element.656), channel_id=1, source_target_pairs={{0,24},{8,16},{16,8},{24,0},{1,25},{9,17},{17,9},{25,1},{2,26},{10... | collective-permute-start | bytes 24584 | tf_op jit(solution)/shard_map/while/body/eval_jaxpr/ppermute | solution.py:319
  165.0 22.4 %all-to-all-start.2 = ((f32[256,1,128]{2,1,0:T(1,128)}), f32[256,1,128]{2,1,0:T(1,128)S(1)}, u32[]{:S(2)}, u32[]{:S(2)}) async-start(f32[256,1,128]{2,1,0:T(1,128)} %bitcast.14), calls=%async_computation.2 | async-start | bytes 262144 | tf_op jit(solution)/shard_map/all_to_all | solution.py:324
  174.6 8.0 %collective-permute-start.20 = (f32[16,128]{1,0:T(8,128)S(1)}, f32[16,128]{1,0:T(8,128)S(1)}, u32[]{:S(2)}, u32[]{:S(2)}) collective-permute-start(f32[16,128]{1,0:T(8,128)S(1)} %get-tuple-element.434), channel_id=1, source_target_pairs={{0,8},{8,0},{16,24},{24,16},{1,9},{9,1},{17,25},{25,17},{2,10},{10... | collective-permute-start | bytes 24584 | tf_op jit(solution)/shard_map/ppermute | solution.py:319
  174.9 12.4 %collective-permute-start.22 = (f32[32,128]{1,0:T(8,128)S(1)}, f32[32,128]{1,0:T(8,128)S(1)}, u32[]{:S(2)}, u32[]{:S(2)}) collective-permute-start(f32[32,128]{1,0:T(8,128)S(1)} %get-tuple-element.436), channel_id=1, source_target_pairs={{0,1},{1,0},{2,3},{3,2},{4,5},{5,4},{6,7},{7,6},{8,9},{9,8},{10,11... | collective-permute-start | bytes 49160 | tf_op jit(solution)/shard_map/ppermute | solution.py:319
  176.9 10.4 %collective-permute-start.23 = (f32[32,128]{1,0:T(8,128)S(1)}, f32[32,128]{1,0:T(8,128)S(1)}, u32[]{:S(2)}, u32[]{:S(2)}) collective-permute-start(f32[32,128]{1,0:T(8,128)S(1)} %get-tuple-element.436), channel_id=1, source_target_pairs={{0,7},{1,2},{2,1},{3,4},{4,3},{5,6},{6,5},{7,0},{8,15},{9,10},{10,... | collective-permute-start | bytes 49160 | tf_op jit(solution)/shard_map/ppermute | solution.py:319
  178.3 9.0 %collective-permute-start.18 = (f32[32,128]{1,0:T(8,128)S(1)}, f32[32,128]{1,0:T(8,128)S(1)}, u32[]{:S(2)}, u32[]{:S(2)}) collective-permute-start(f32[32,128]{1,0:T(8,128)S(1)} %get-tuple-element.432), channel_id=1, source_target_pairs={{0,32},{32,0},{64,96},{96,64},{128,160},{160,128},{192,224},{224,1... | collective-permute-start | bytes 49160 | tf_op jit(solution)/shard_map/ppermute | solution.py:319
  179.8 7.5 %collective-permute-start.19 = (f32[32,128]{1,0:T(8,128)S(1)}, f32[32,128]{1,0:T(8,128)S(1)}, u32[]{:S(2)}, u32[]{:S(2)}) collective-permute-start(f32[32,128]{1,0:T(8,128)S(1)} %get-tuple-element.433), channel_id=1, source_target_pairs={{0,224},{32,64},{64,32},{96,128},{128,96},{160,192},{192,160},{224... | collective-permute-start | bytes 49160 | tf_op jit(solution)/shard_map/ppermute | solution.py:319
  182.7 4.6 %collective-permute-start.21 = (f32[16,128]{1,0:T(8,128)S(1)}, f32[16,128]{1,0:T(8,128)S(1)}, u32[]{:S(2)}, u32[]{:S(2)}) collective-permute-start(f32[16,128]{1,0:T(8,128)S(1)} %get-tuple-element.435), channel_id=1, source_target_pairs={{0,24},{8,16},{16,8},{24,0},{1,25},{9,17},{17,9},{25,1},{2,26},{10... | collective-permute-start | bytes 24584 | tf_op jit(solution)/shard_map/ppermute | solution.py:319
  212.2 18.7 %all-to-all-start.4 = ((f32[256,1,128]{2,1,0:T(1,128)}), f32[256,1,128]{2,1,0:T(1,128)S(1)}, u32[]{:S(2)}, u32[]{:S(2)}) async-start(f32[256,1,128]{2,1,0:T(1,128)} %bitcast.20), calls=%async_computation.4 | async-start | bytes 262144 | tf_op jit(solution)/shard_map/all_to_all | solution.py:324
where the time goes:
time: 234 us; the launch traced here: 231 us
  starting transfers between devices  154 us (66%)
  Pallas kernels  36.4 us (16%)
  blocking collectives  22.1 us (9%)
  waiting for transfers between devices  17.5 us (7%)
    ppermute x48, starting transfers between devices, swap(): got.append(lax.ppermute(block, axis, pairs))  79.6 us
    all_to_all x8, starting transfers between devices, spread(): return lax.all_to_all(sent, AXES, 0, 0, tiled=True)  74.3 us
    pallas_call x20, Pallas kernels, call(): pl.pallas_call(kernel, out_shape=[pltpu.HBM(shape, F32) if i in far_out e...  36.4 us
    all_to_all x1, blocking collectives, spread(): return lax.all_to_all(sent, AXES, 0, 0, tiled=True)  22.1 us
    all_to_all x8, waiting for transfers between devices, spread(): return lax.all_to_all(sent, AXES, 0, 0, tiled=True)  9.99 us
    ppermute x48, waiting for transfers between devices, swap(): got.append(lax.ppermute(block, axis, pairs))  7.49 us
  transfers between devices with their start and end apart: 56, of which 9 were waited for; matrix products, arithmetic and copies ran while one was open for 0% of the time, Pallas kernels for 7%

commit v1 on v0

--- a/solution.py
+++ b/solution.py
@@ -189,7 +189,7 @@
     column[p] = column[p] * flip(column_halo(where, z_one[...], z_two[...]))
 
 
-def rates(act, where, spin, side, column, odds, gain, h, a, v, x_one, x_two, y_one, y_two, zed, sent):
+def rates(act, where, spin, side, column, odds, gain, h, a, v, x_one, x_two, y_one, y_two, zed, sent, row, leaves):
     p = 1 - act
     lane = lane_of()
     one_row = lane_of(1)
@@ -202,7 +202,7 @@
     top = lax.broadcasted_iota(jnp.int32, (HY, BZ), 0) == 0
 
     def step(i, carry):
-        packed, summed = carry
+        summed = carry
         for j in range(UNROLL):
             x = i * UNROLL + j
             odd = odd_row(j + act)
@@ -216,13 +216,19 @@
             gain[x] = g
             grown = 1.0 + jnp.exp(2.0 * spin[act, x + 1, :HY] * g)
             summed = summed + a[act, x] / grown
-            root = v[x] * grown
-            square = root * root
-            odds[x] = square
-            packed = add_face(packed, square, x, odd)
-        return packed, summed
-
-    packed, summed = lax.fori_loop(0, BX // UNROLL, step, (jnp.zeros((HY, BZ), F32), jnp.zeros((HY, BZ), F32)))
+            odds[x] = grown
+        return summed
+
+    summed = lax.fori_loop(0, BX // UNROLL, step, jnp.zeros((HY, BZ), F32))
+    row[...] = jnp.broadcast_to(jnp.sum(summed, axis=0, keepdims=True), row.shape)
+    leaving = pltpu.make_async_copy(row, sent, leaves)
+    leaving.start()
+    packed = jnp.zeros((HY, BZ), F32)
+    for x in range(BX):
+        root = v[x] * odds[x]
+        square = root * root
+        odds[x] = square
+        packed = add_face(packed, square, x, odd_row(x + act))
     x_one[...] = odds[far_or_near(where[1], BX - 1, 0)]
     x_two[...] = odds[far_or_near(where[1], 0, BX - 1)]
     one, two = far_or_near(where[2], HY - 1, 0), far_or_near(where[2], 0, HY - 1)
@@ -230,12 +236,12 @@
         y_one[x : x + 1] = odds[x, pl.ds(one, 1)]
         y_two[x : x + 1] = odds[x, pl.ds(two, 1)]
     zed[...] = packed
-    sent[...] = jnp.broadcast_to(jnp.sum(summed, axis=0, keepdims=True), sent.shape)
+    leaving.wait()
 
 
 def first_kernel(
     where, from_x_one, from_x_two, from_y_one, from_y_two, from_z_one, from_z_two, h, a, v, spin_in,
-    spin, side, column, energy, fields, clock, odds, gain, x_one, x_two, y_one, y_two, zed, sent,
+    spin, side, column, energy, fields, clock, odds, gain, x_one, x_two, y_one, y_two, zed, sent, row, leaves,
 ):
     for p in range(2):
         spin[p, far_or_near(where[1], BX + 1, 0), :HY] = from_x_one[p]
@@ -249,18 +255,18 @@
     fields[1] = eighth(of_field)
     energy[...] = jnp.zeros(energy.shape, F32)
     clock[...] = jnp.zeros(clock.shape, F32)
-    rates(0, where, spin, side, column, odds, gain, h, a, v, x_one, x_two, y_one, y_two, zed, sent)
+    rates(0, where, spin, side, column, odds, gain, h, a, v, x_one, x_two, y_one, y_two, zed, sent, row, leaves)
 
 
 def section_kernel(
     act, half, where, gathered, from_x_one, from_x_two, from_y_one, from_y_two, from_z_one, from_z_two, h, a, v,
     spin_in, side_in, column_in, energy_in, fields_in, clock_in, odds_in, gain_in,
-    spin, side, column, energy, fields, clock, odds, gain, x_one, x_two, y_one, y_two, zed, sent,
+    spin, side, column, energy, fields, clock, odds, gain, x_one, x_two, y_one, y_two, zed, sent, row, leaves,
 ):
     k = where[0]
     halo = (where, from_x_one, from_x_two, from_y_one, from_y_two, from_z_one, from_z_two)
     advance(k, 1 - act, half, gathered, halo, spin, side, column, odds, gain, h, energy, fields, clock)
-    rates(act, where, spin, side, column, odds, gain, h, a, v, x_one, x_two, y_one, y_two, zed, sent)
+    rates(act, where, spin, side, column, odds, gain, h, a, v, x_one, x_two, y_one, y_two, zed, sent, row, leaves)
 
 
 def last_kernel(
@@ -351,7 +357,10 @@
         fields_kernel, (site_field, attempt_rate, uniforms), [(2, *block), (2, *block), block],
         far=(0, 1, 2), scratch=[brick, brick, drawn, dma((3,))],
     )
-    carried = call(first_kernel, (where(0), *halo, h, a, v, spin), state + faces + [sent_shape], {10: 0})
+    carried = call(
+        first_kernel, (where(0), *halo, h, a, v, spin), state + faces + [sent_shape], {10: 0},
+        far_out=(len(state) + len(faces),), scratch=[pltpu.VMEM(sent_shape, F32), dma],
+    )
 
     def section(k, act, carried):
         *kept, x_one, x_two, y_one, y_two, zed, sent = carried
@@ -364,7 +373,8 @@
         return call(
             functools.partial(section_kernel, act, half),
             (where(k), gathered, *halo, h, a, v, *kept), state + faces + [sent_shape],
-            {11 + i: i for i in range(len(state))},
+            {11 + i: i for i in range(len(state))}, far_out=(len(state) + len(faces),),
+            scratch=[pltpu.VMEM(sent_shape, F32), dma],
         )
 
     def pair(i, carried):

time: 234 us -> 235 us (level)
  no operation moved by 1% of the time
where the time goes in v1:
time: 235 us; the launch traced here: 232 us
  starting transfers between devices  154 us (66%)
  Pallas kernels  36.6 us (16%)
  blocking collectives  22.2 us (9%)
  waiting for transfers between devices  17.5 us (7%)
    ppermute x48, starting transfers between devices, swap(): got.append(lax.ppermute(block, axis, pairs))  79.6 us
    all_to_all x8, starting transfers between devices, spread(): return lax.all_to_all(sent, AXES, 0, 0, tiled=True)  74.3 us
    pallas_call x20, Pallas kernels, call(): pl.pallas_call(kernel, out_shape=[pltpu.HBM(shape, F32) if i in far_out e...  36.6 us
    all_to_all x1, blocking collectives, spread(): return lax.all_to_all(sent, AXES, 0, 0, tiled=True)  22.2 us
    all_to_all x8, waiting for transfers between devices, spread(): return lax.all_to_all(sent, AXES, 0, 0, tiled=True)  9.99 us
    ppermute x48, waiting for transfers between devices, swap(): got.append(lax.ppermute(block, axis, pairs))  7.49 us
  transfers between devices with their start and end apart: 56, of which 9 were waited for; matrix products, arithmetic and copies ran while one was open for 0% of the time, Pallas kernels for 7%

profile of v1, /device:TPU:32, one launch (start us, length us, event | category | flops | bytes accessed | tf_op | source)
XLA Modules:
  0.0 231.9 jit_solution(9318670164895500343)
XLA Ops:
  0.7 2.7 %shard_map.59 = (f32[2,18,40,128]{3,2,1,0:T(8,128)S(1)}, f32[2,32,128]{2,1,0:T(8,128)S(1)}, f32[2,32,128]{2,1,0:T(8,128)S(1)}, f32[2,16,128]{2,1,0:T(8,128)S(1)}...) custom-call(s32[4]{0:T(128)S(1)} %add_add_fusion.3.where, s32[16,64,128]{2,1,0:T(8,128)} %occ_hbm.1), custom_call_target="tpu_custom_call" | custom-call | flops 1000000 | bytes 1000000 | tf_op jit(solution)/shard_map/pallas_call | solution.py:307
  3.6 1.6 collective-permute-start.12
  5.2 3.0 %collective-permute-start.13 = (f32[2,32,128]{2,1,0:T(8,128)S(1)}, f32[2,32,128]{2,1,0:T(8,128)S(1)}, u32[]{:S(2)}, u32[]{:S(2)}) collective-permute-start(f32[2,32,128]{2,1,0:T(8,128)S(1)} %get-tuple-element.409), channel_id=1, source_target_pairs={{0,224},{32,64},{64,32},{96,128},{128,96},{160,192},{192,160},{224... | collective-permute-start | bytes 98312 | tf_op jit(solution)/shard_map/ppermute | solution.py:325
  8.3 3.7 %collective-permute-start.17 = (f32[2,32,128]{2,1,0:T(8,128)S(1)}, f32[2,32,128]{2,1,0:T(8,128)S(1)}, u32[]{:S(2)}, u32[]{:S(2)}) collective-permute-start(f32[2,32,128]{2,1,0:T(8,128)S(1)} %get-tuple-element.412), channel_id=1, source_target_pairs={{0,7},{1,2},{2,1},{3,4},{4,3},{5,6},{6,5},{7,0},{8,15},{9,10},{10,... | collective-permute-start | bytes 98312 | tf_op jit(solution)/shard_map/ppermute | solution.py:325
  12.0 1.9 collective-permute-start.15
  13.9 2.0 shard_map.60
  16.8 2.2 shard_map.61
  19.0 145.7 %while.39 = (s32[]{:T(128)}, f32[2,18,40,128]{3,2,1,0:T(8,128)S(1)}, f32[2,16,128]{2,1,0:T(8,128)S(1)}, f32[2,32,128]{2,1,0:T(8,128)S(1)}, f32[8,8,128]{2,1,0:T(...) while((s32[]{:T(128)}, ...), condition=%wide.region_1.2_spmd, body=%wide.region_0.1_spmd.sunk | while | flops 4000029 | bytes 5442641 | solution.py:383
  19.0 10.0 %all-to-all-start = ((f32[256,1,128]{2,1,0:T(1,128)}), f32[256,1,128]{2,1,0:T(1,128)S(1)}, u32[]{:S(2)}, u32[]{:S(2)}) async-start(f32[256,1,128]{2,1,0:T(1,128)} %bitcast.47), calls=%async_computation | async-start | bytes 262144 | tf_op jit(solution)/shard_map/while/body/eval_jaxpr/all_to_all | solution.py:330
  29.3 2.0 collective-permute-start.4
  31.3 1.5 collective-permute-start.5
  32.7 1.5 collective-permute-start
  34.2 2.9 %collective-permute-start.1 = (f32[32,128]{1,0:T(8,128)S(1)}, f32[32,128]{1,0:T(8,128)S(1)}, u32[]{:S(2)}, u32[]{:S(2)}) collective-permute-start(f32[32,128]{1,0:T(8,128)S(1)} %get-tuple-element.713), channel_id=1, source_target_pairs={{0,224},{32,64},{64,32},{96,128},{128,96},{160,192},{192,160},{224... | collective-permute-start | bytes 49160 | tf_op jit(solution)/shard_map/while/body/eval_jaxpr/ppermute | solution.py:325
  37.1 1.9 collective-permute-start.3
  39.0 1.7 eval_jaxpr.12.v
  41.7 1.8 eval_jaxpr.13
  43.6 9.7 %all-to-all-start.1 = ((f32[256,1,128]{2,1,0:T(1,128)}), f32[256,1,128]{2,1,0:T(1,128)S(1)}, u32[]{:S(2)}, u32[]{:S(2)}) async-start(f32[256,1,128]{2,1,0:T(1,128)} %bitcast.49), calls=%async_computation.1 | async-start | bytes 262144 | tf_op jit(solution)/shard_map/while/body/eval_jaxpr/all_to_all | solution.py:330
  53.5 2.0 collective-permute-start.10
  56.9 1.5 collective-permute-start.6
  58.4 2.9 %collective-permute-start.7 = (f32[32,128]{1,0:T(8,128)S(1)}, f32[32,128]{1,0:T(8,128)S(1)}, u32[]{:S(2)}, u32[]{:S(2)}) collective-permute-start(f32[32,128]{1,0:T(8,128)S(1)} %get-tuple-element.654), channel_id=1, source_target_pairs={{0,224},{32,64},{64,32},{96,128},{128,96},{160,192},{192,160},{224... | collective-permute-start | bytes 49160 | tf_op jit(solution)/shard_map/while/body/eval_jaxpr/ppermute | solution.py:325
  61.3 1.9 collective-permute-start.9
  63.2 1.7 eval_jaxpr.14.v
  65.9 1.8 eval_jaxpr.15
  67.8 9.7 %all-to-all-start = ((f32[256,1,128]{2,1,0:T(1,128)}), f32[256,1,128]{2,1,0:T(1,128)S(1)}, u32[]{:S(2)}, u32[]{:S(2)}) async-start(f32[256,1,128]{2,1,0:T(1,128)} %bitcast.47), calls=%async_computation | async-start | bytes 262144 | tf_op jit(solution)/shard_map/while/body/eval_jaxpr/all_to_all | solution.py:330
  77.7 2.0 collective-permute-start.4
  79.7 1.5 collective-permute-start.5
  81.2 1.5 collective-permute-start
  82.7 2.9 %collective-permute-start.1 = (f32[32,128]{1,0:T(8,128)S(1)}, f32[32,128]{1,0:T(8,128)S(1)}, u32[]{:S(2)}, u32[]{:S(2)}) collective-permute-start(f32[32,128]{1,0:T(8,128)S(1)} %get-tuple-element.713), channel_id=1, source_target_pairs={{0,224},{32,64},{64,32},{96,128},{128,96},{160,192},{192,160},{224... | collective-permute-start | bytes 49160 | tf_op jit(solution)/shard_map/while/body/eval_jaxpr/ppermute | solution.py:325
  85.5 1.9 collective-permute-start.3
  87.5 1.7 eval_jaxpr.12.v
  90.2 1.8 eval_jaxpr.13
  92.0 9.7 %all-to-all-start.1 = ((f32[256,1,128]{2,1,0:T(1,128)}), f32[256,1,128]{2,1,0:T(1,128)S(1)}, u32[]{:S(2)}, u32[]{:S(2)}) async-start(f32[256,1,128]{2,1,0:T(1,128)} %bitcast.49), calls=%async_computation.1 | async-start | bytes 262144 | tf_op jit(solution)/shard_map/while/body/eval_jaxpr/all_to_all | solution.py:330
  101.9 2.0 collective-permute-start.10
  105.4 1.5 collective-permute-start.6
  106.9 2.9 %collective-permute-start.7 = (f32[32,128]{1,0:T(8,128)S(1)}, f32[32,128]{1,0:T(8,128)S(1)}, u32[]{:S(2)}, u32[]{:S(2)}) collective-permute-start(f32[32,128]{1,0:T(8,128)S(1)} %get-tuple-element.654), channel_id=1, source_target_pairs={{0,224},{32,64},{64,32},{96,128},{128,96},{160,192},{192,160},{224... | collective-permute-start | bytes 49160 | tf_op jit(solution)/shard_map/while/body/eval_jaxpr/ppermute | solution.py:325
  109.7 1.9 collective-permute-start.9
  111.7 1.7 eval_jaxpr.14.v
  114.4 1.8 eval_jaxpr.15
  116.3 9.7 %all-to-all-start = ((f32[256,1,128]{2,1,0:T(1,128)}), f32[256,1,128]{2,1,0:T(1,128)S(1)}, u32[]{:S(2)}, u32[]{:S(2)}) async-start(f32[256,1,128]{2,1,0:T(1,128)} %bitcast.47), calls=%async_computation | async-start | bytes 262144 | tf_op jit(solution)/shard_map/while/body/eval_jaxpr/all_to_all | solution.py:330
  126.2 2.0 collective-permute-start.4
  128.2 1.5 collective-permute-start.5
  129.6 1.5 collective-permute-start
  131.1 2.9 %collective-permute-start.1 = (f32[32,128]{1,0:T(8,128)S(1)}, f32[32,128]{1,0:T(8,128)S(1)}, u32[]{:S(2)}, u32[]{:S(2)}) collective-permute-start(f32[32,128]{1,0:T(8,128)S(1)} %get-tuple-element.713), channel_id=1, source_target_pairs={{0,224},{32,64},{64,32},{96,128},{128,96},{160,192},{192,160},{224... | collective-permute-start | bytes 49160 | tf_op jit(solution)/shard_map/while/body/eval_jaxpr/ppermute | solution.py:325
  134.0 1.9 collective-permute-start.3
  135.9 1.7 eval_jaxpr.12.v
  138.6 1.8 eval_jaxpr.13
  140.5 9.7 %all-to-all-start.1 = ((f32[256,1,128]{2,1,0:T(1,128)}), f32[256,1,128]{2,1,0:T(1,128)S(1)}, u32[]{:S(2)}, u32[]{:S(2)}) async-start(f32[256,1,128]{2,1,0:T(1,128)} %bitcast.49), calls=%async_computation.1 | async-start | bytes 262144 | tf_op jit(solution)/shard_map/while/body/eval_jaxpr/all_to_all | solution.py:330
  150.4 2.0 collective-permute-start.10
  153.8 1.5 collective-permute-start.6
  155.3 2.9 %collective-permute-start.7 = (f32[32,128]{1,0:T(8,128)S(1)}, f32[32,128]{1,0:T(8,128)S(1)}, u32[]{:S(2)}, u32[]{:S(2)}) collective-permute-start(f32[32,128]{1,0:T(8,128)S(1)} %get-tuple-element.654), channel_id=1, source_target_pairs={{0,224},{32,64},{64,32},{96,128},{128,96},{160,192},{192,160},{224... | collective-permute-start | bytes 49160 | tf_op jit(solution)/shard_map/while/body/eval_jaxpr/ppermute | solution.py:325
  158.2 1.9 collective-permute-start.9
  160.1 1.7 eval_jaxpr.14.v
  162.8 1.8 eval_jaxpr.15
  164.7 9.7 %all-to-all-start.2 = ((f32[256,1,128]{2,1,0:T(1,128)}), f32[256,1,128]{2,1,0:T(1,128)S(1)}, u32[]{:S(2)}, u32[]{:S(2)}) async-start(f32[256,1,128]{2,1,0:T(1,128)} %bitcast.48), calls=%async_computation.2 | async-start | bytes 262144 | tf_op jit(solution)/shard_map/all_to_all | solution.py:330
  174.6 2.0 collective-permute-start.22
  178.1 1.5 collective-permute-start.18
  179.6 2.9 %collective-permute-start.19 = (f32[32,128]{1,0:T(8,128)S(1)}, f32[32,128]{1,0:T(8,128)S(1)}, u32[]{:S(2)}, u32[]{:S(2)}) collective-permute-start(f32[32,128]{1,0:T(8,128)S(1)} %get-tuple-element.433), channel_id=1, source_target_pairs={{0,224},{32,64},{64,32},{96,128},{128,96},{160,192},{192,160},{224... | collective-permute-start | bytes 49160 | tf_op jit(solution)/shard_map/ppermute | solution.py:325
  182.4 1.9 collective-permute-start.21
  184.4 1.7 shard_map.62.v
  187.1 2.5 %shard_map.63 = (f32[2,18,40,128]{3,2,1,0:T(8,128)S(1)}, f32[2,16,128]{2,1,0:T(8,128)S(1)}, f32[2,32,128]{2,1,0:T(8,128)S(1)}, f32[8,8,128]{2,1,0:T(8,128)S(1)},...) custom-call(s32[4]{0:T(128)S(1)} %add_add_fusion.2.where, ...), custom_call_target="tpu_custom_call", output_to_operand_aliasing={{0}: (11, {}), {1}: (12, {}), {2}: (13, {}), {3}: (14, {}),... | custom-call | flops 1000000 | bytes 1000000 | tf_op jit(solution)/shard_map/pallas_call | solution.py:307
  189.5 22.2 %all_to_all.53 = f32[256,1,128]{2,1,0:T(1,128)S(1)} all-to-all(f32[256,1,128]{2,1,0:T(1,128)} %bitcast.50), channel_id=1, replica_groups=mesh['gx'=8,'gy'=4,'gz'=8] {'gx','gy','gz'}, dimensions={0} | all-to-all | bytes 262144 | tf_op jit(solution)/shard_map/all_to_all | solution.py:330
  212.7 6.1 %all-to-all-start.4 = ((f32[256,1,128]{2,1,0:T(1,128)}), f32[256,1,128]{2,1,0:T(1,128)S(1)}, u32[]{:S(2)}, u32[]{:S(2)}) async-start(f32[256,1,128]{2,1,0:T(1,128)} %bitcast.20), calls=%async_computation.4 | async-start | bytes 262144 | tf_op jit(solution)/shard_map/all_to_all | solution.py:330
  218.8 2.6 %shard_map.65 = f32[16,64,128]{2,1,0:T(8,128)} custom-call(f32[2,18,40,128]{3,2,1,0:T(8,128)S(1)} %get-tuple-element.452.spin), custom_call_target="tpu_custom_call" | custom-call | flops 1000000 | bytes 1000000 | tf_op jit(solution)/shard_map/pallas_call | solution.py:307
  221.4 10.0 %all-to-all-done.4 = f32[256,1,128]{2,1,0:T(1,128)S(1)} async-done(((f32[256,1,128]{2,1,0:T(1,128)}), f32[256,1,128]{2,1,0:T(1,128)S(1)}, u32[]{:S(2)}, u32[]{:S(2)}) %all-to-all-start.4) | async-done | bytes 131104 | tf_op jit(solution)/shard_map/all_to_all | solution.py:330
  (78 shorter events, 17.2 us)
Async XLA Ops:
  3.5 8.5 %collective-permute-start.14 = (f32[2,16,128]{2,1,0:T(8,128)S(1)}, f32[2,16,128]{2,1,0:T(8,128)S(1)}, u32[]{:S(2)}, u32[]{:S(2)}) collective-permute-start(f32[2,16,128]{2,1,0:T(8,128)S(1)} %get-tuple-element.410), channel_id=1, source_target_pairs={{0,8},{8,0},{16,24},{24,16},{1,9},{9,1},{17,25},{25,17},{2,10},{10... | collective-permute-start | bytes 49160 | tf_op jit(solution)/shard_map/ppermute | solution.py:325
  3.6 13.2 %collective-permute-start.12 = (f32[2,32,128]{2,1,0:T(8,128)S(1)}, f32[2,32,128]{2,1,0:T(8,128)S(1)}, u32[]{:S(2)}, u32[]{:S(2)}) collective-permute-start(f32[2,32,128]{2,1,0:T(8,128)S(1)} %get-tuple-element.408), channel_id=1, source_target_pairs={{0,32},{32,0},{64,96},{96,64},{128,160},{160,128},{192,224},{224,1... | collective-permute-start | bytes 98312 | tf_op jit(solution)/shard_map/ppermute | solution.py:325
  5.2 11.6 %collective-permute-start.13 = (f32[2,32,128]{2,1,0:T(8,128)S(1)}, f32[2,32,128]{2,1,0:T(8,128)S(1)}, u32[]{:S(2)}, u32[]{:S(2)}) collective-permute-start(f32[2,32,128]{2,1,0:T(8,128)S(1)} %get-tuple-element.409), channel_id=1, source_target_pairs={{0,224},{32,64},{64,32},{96,128},{128,96},{160,192},{192,160},{224... | collective-permute-start | bytes 98312 | tf_op jit(solution)/shard_map/ppermute | solution.py:325
  8.2 8.6 %collective-permute-start.16 = (f32[2,32,128]{2,1,0:T(8,128)S(1)}, f32[2,32,128]{2,1,0:T(8,128)S(1)}, u32[]{:S(2)}, u32[]{:S(2)}) collective-permute-start(f32[2,32,128]{2,1,0:T(8,128)S(1)} %get-tuple-element.412), channel_id=1, source_target_pairs={{0,1},{1,0},{2,3},{3,2},{4,5},{5,4},{6,7},{7,6},{8,9},{9,8},{10,11... | collective-permute-start | bytes 98312 | tf_op jit(solution)/shard_map/ppermute | solution.py:325
  8.3 8.5 %collective-permute-start.17 = (f32[2,32,128]{2,1,0:T(8,128)S(1)}, f32[2,32,128]{2,1,0:T(8,128)S(1)}, u32[]{:S(2)}, u32[]{:S(2)}) collective-permute-start(f32[2,32,128]{2,1,0:T(8,128)S(1)} %get-tuple-element.412), channel_id=1, source_target_pairs={{0,7},{1,2},{2,1},{3,4},{4,3},{5,6},{6,5},{7,0},{8,15},{9,10},{10,... | collective-permute-start | bytes 98312 | tf_op jit(solution)/shard_map/ppermute | solution.py:325
  12.0 4.8 %collective-permute-start.15 = (f32[2,16,128]{2,1,0:T(8,128)S(1)}, f32[2,16,128]{2,1,0:T(8,128)S(1)}, u32[]{:S(2)}, u32[]{:S(2)}) collective-permute-start(f32[2,16,128]{2,1,0:T(8,128)S(1)} %get-tuple-element.411), channel_id=1, source_target_pairs={{0,24},{8,16},{16,8},{24,0},{1,25},{9,17},{17,9},{25,1},{2,26},{10... | collective-permute-start | bytes 49160 | tf_op jit(solution)/shard_map/ppermute | solution.py:325
  19.0 22.7 %all-to-all-start = ((f32[256,1,128]{2,1,0:T(1,128)}), f32[256,1,128]{2,1,0:T(1,128)S(1)}, u32[]{:S(2)}, u32[]{:S(2)}) async-start(f32[256,1,128]{2,1,0:T(1,128)} %bitcast.47), calls=%async_computation | async-start | bytes 262144 | tf_op jit(solution)/shard_map/while/body/eval_jaxpr/all_to_all | solution.py:330
  29.0 8.0 %collective-permute-start.2 = (f32[16,128]{1,0:T(8,128)S(1)}, f32[16,128]{1,0:T(8,128)S(1)}, u32[]{:S(2)}, u32[]{:S(2)}) collective-permute-start(f32[16,128]{1,0:T(8,128)S(1)} %get-tuple-element.714), channel_id=1, source_target_pairs={{0,8},{8,0},{16,24},{24,16},{1,9},{9,1},{17,25},{25,17},{2,10},{10... | collective-permute-start | bytes 24584 | tf_op jit(solution)/shard_map/while/body/eval_jaxpr/ppermute | solution.py:325
  29.3 12.4 %collective-permute-start.4 = (f32[32,128]{1,0:T(8,128)S(1)}, f32[32,128]{1,0:T(8,128)S(1)}, u32[]{:S(2)}, u32[]{:S(2)}) collective-permute-start(f32[32,128]{1,0:T(8,128)S(1)} %get-tuple-element.716), channel_id=1, source_target_pairs={{0,1},{1,0},{2,3},{3,2},{4,5},{5,4},{6,7},{7,6},{8,9},{9,8},{10,11... | collective-permute-start | bytes 49160 | tf_op jit(solution)/shard_map/while/body/eval_jaxpr/ppermute | solution.py:325
  31.3 10.4 %collective-permute-start.5 = (f32[32,128]{1,0:T(8,128)S(1)}, f32[32,128]{1,0:T(8,128)S(1)}, u32[]{:S(2)}, u32[]{:S(2)}) collective-permute-start(f32[32,128]{1,0:T(8,128)S(1)} %get-tuple-element.716), channel_id=1, source_target_pairs={{0,7},{1,2},{2,1},{3,4},{4,3},{5,6},{6,5},{7,0},{8,15},{9,10},{10,... | collective-permute-start | bytes 49160 | tf_op jit(solution)/shard_map/while/body/eval_jaxpr/ppermute | solution.py:325
  32.7 9.0 %collective-permute-start = (f32[32,128]{1,0:T(8,128)S(1)}, f32[32,128]{1,0:T(8,128)S(1)}, u32[]{:S(2)}, u32[]{:S(2)}) collective-permute-start(f32[32,128]{1,0:T(8,128)S(1)} %get-tuple-element.712), channel_id=1, source_target_pairs={{0,32},{32,0},{64,96},{96,64},{128,160},{160,128},{192,224},{224,1... | collective-permute-start | bytes 49160 | tf_op jit(solution)/shard_map/while/body/eval_jaxpr/ppermute | solution.py:325
  34.2 7.5 %collective-permute-start.1 = (f32[32,128]{1,0:T(8,128)S(1)}, f32[32,128]{1,0:T(8,128)S(1)}, u32[]{:S(2)}, u32[]{:S(2)}) collective-permute-start(f32[32,128]{1,0:T(8,128)S(1)} %get-tuple-element.713), channel_id=1, source_target_pairs={{0,224},{32,64},{64,32},{96,128},{128,96},{160,192},{192,160},{224... | collective-permute-start | bytes 49160 | tf_op jit(solution)/shard_map/while/body/eval_jaxpr/ppermute | solution.py:325
  37.1 4.6 %collective-permute-start.3 = (f32[16,128]{1,0:T(8,128)S(1)}, f32[16,128]{1,0:T(8,128)S(1)}, u32[]{:S(2)}, u32[]{:S(2)}) collective-permute-start(f32[16,128]{1,0:T(8,128)S(1)} %get-tuple-element.715), channel_id=1, source_target_pairs={{0,24},{8,16},{16,8},{24,0},{1,25},{9,17},{17,9},{25,1},{2,26},{10... | collective-permute-start | bytes 24584 | tf_op jit(solution)/shard_map/while/body/eval_jaxpr/ppermute | solution.py:325
  43.6 22.4 %all-to-all-start.1 = ((f32[256,1,128]{2,1,0:T(1,128)}), f32[256,1,128]{2,1,0:T(1,128)S(1)}, u32[]{:S(2)}, u32[]{:S(2)}) async-start(f32[256,1,128]{2,1,0:T(1,128)} %bitcast.49), calls=%async_computation.1 | async-start | bytes 262144 | tf_op jit(solution)/shard_map/while/body/eval_jaxpr/all_to_all | solution.py:330
  53.3 8.0 %collective-permute-start.8 = (f32[16,128]{1,0:T(8,128)S(1)}, f32[16,128]{1,0:T(8,128)S(1)}, u32[]{:S(2)}, u32[]{:S(2)}) collective-permute-start(f32[16,128]{1,0:T(8,128)S(1)} %get-tuple-element.655), channel_id=1, source_target_pairs={{0,8},{8,0},{16,24},{24,16},{1,9},{9,1},{17,25},{25,17},{2,10},{10... | collective-permute-start | bytes 24584 | tf_op jit(solution)/shard_map/while/body/eval_jaxpr/ppermute | solution.py:325
  53.5 12.4 %collective-permute-start.10 = (f32[32,128]{1,0:T(8,128)S(1)}, f32[32,128]{1,0:T(8,128)S(1)}, u32[]{:S(2)}, u32[]{:S(2)}) collective-permute-start(f32[32,128]{1,0:T(8,128)S(1)} %get-tuple-element.657), channel_id=1, source_target_pairs={{0,1},{1,0},{2,3},{3,2},{4,5},{5,4},{6,7},{7,6},{8,9},{9,8},{10,11... | collective-permute-start | bytes 49160 | tf_op jit(solution)/shard_map/while/body/eval_jaxpr/ppermute | solution.py:325
  55.5 10.4 %collective-permute-start.11 = (f32[32,128]{1,0:T(8,128)S(1)}, f32[32,128]{1,0:T(8,128)S(1)}, u32[]{:S(2)}, u32[]{:S(2)}) collective-permute-start(f32[32,128]{1,0:T(8,128)S(1)} %get-tuple-element.657), channel_id=1, source_target_pairs={{0,7},{1,2},{2,1},{3,4},{4,3},{5,6},{6,5},{7,0},{8,15},{9,10},{10,... | collective-permute-start | bytes 49160 | tf_op jit(solution)/shard_map/while/body/eval_jaxpr/ppermute | solution.py:325
  56.9 9.0 %collective-permute-start.6 = (f32[32,128]{1,0:T(8,128)S(1)}, f32[32,128]{1,0:T(8,128)S(1)}, u32[]{:S(2)}, u32[]{:S(2)}) collective-permute-start(f32[32,128]{1,0:T(8,128)S(1)} %get-tuple-element.653), channel_id=1, source_target_pairs={{0,32},{32,0},{64,96},{96,64},{128,160},{160,128},{192,224},{224,1... | collective-permute-start | bytes 49160 | tf_op jit(solution)/shard_map/while/body/eval_jaxpr/ppermute | solution.py:325
  58.4 7.5 %collective-permute-start.7 = (f32[32,128]{1,0:T(8,128)S(1)}, f32[32,128]{1,0:T(8,128)S(1)}, u32[]{:S(2)}, u32[]{:S(2)}) collective-permute-start(f32[32,128]{1,0:T(8,128)S(1)} %get-tuple-element.654), channel_id=1, source_target_pairs={{0,224},{32,64},{64,32},{96,128},{128,96},{160,192},{192,160},{224... | collective-permute-start | bytes 49160 | tf_op jit(solution)/shard_map/while/body/eval_jaxpr/ppermute | solution.py:325
  61.3 4.6 %collective-permute-start.9 = (f32[16,128]{1,0:T(8,128)S(1)}, f32[16,128]{1,0:T(8,128)S(1)}, u32[]{:S(2)}, u32[]{:S(2)}) collective-permute-start(f32[16,128]{1,0:T(8,128)S(1)} %get-tuple-element.656), channel_id=1, source_target_pairs={{0,24},{8,16},{16,8},{24,0},{1,25},{9,17},{17,9},{25,1},{2,26},{10... | collective-permute-start | bytes 24584 | tf_op jit(solution)/shard_map/while/body/eval_jaxpr/ppermute | solution.py:325
  67.8 22.4 %all-to-all-start = ((f32[256,1,128]{2,1,0:T(1,128)}), f32[256,1,128]{2,1,0:T(1,128)S(1)}, u32[]{:S(2)}, u32[]{:S(2)}) async-start(f32[256,1,128]{2,1,0:T(1,128)} %bitcast.47), calls=%async_computation | async-start | bytes 262144 | tf_op jit(solution)/shard_map/while/body/eval_jaxpr/all_to_all | solution.py:330
  77.5 8.0 %collective-permute-start.2 = (f32[16,128]{1,0:T(8,128)S(1)}, f32[16,128]{1,0:T(8,128)S(1)}, u32[]{:S(2)}, u32[]{:S(2)}) collective-permute-start(f32[16,128]{1,0:T(8,128)S(1)} %get-tuple-element.714), channel_id=1, source_target_pairs={{0,8},{8,0},{16,24},{24,16},{1,9},{9,1},{17,25},{25,17},{2,10},{10... | collective-permute-start | bytes 24584 | tf_op jit(solution)/shard_map/while/body/eval_jaxpr/ppermute | solution.py:325
  77.7 12.4 %collective-permute-start.4 = (f32[32,128]{1,0:T(8,128)S(1)}, f32[32,128]{1,0:T(8,128)S(1)}, u32[]{:S(2)}, u32[]{:S(2)}) collective-permute-start(f32[32,128]{1,0:T(8,128)S(1)} %get-tuple-element.716), channel_id=1, source_target_pairs={{0,1},{1,0},{2,3},{3,2},{4,5},{5,4},{6,7},{7,6},{8,9},{9,8},{10,11... | collective-permute-start | bytes 49160 | tf_op jit(solution)/shard_map/while/body/eval_jaxpr/ppermute | solution.py:325
  79.7 10.4 %collective-permute-start.5 = (f32[32,128]{1,0:T(8,128)S(1)}, f32[32,128]{1,0:T(8,128)S(1)}, u32[]{:S(2)}, u32[]{:S(2)}) collective-permute-start(f32[32,128]{1,0:T(8,128)S(1)} %get-tuple-element.716), channel_id=1, source_target_pairs={{0,7},{1,2},{2,1},{3,4},{4,3},{5,6},{6,5},{7,0},{8,15},{9,10},{10,... | collective-permute-start | bytes 49160 | tf_op jit(solution)/shard_map/while/body/eval_jaxpr/ppermute | solution.py:325
  81.2 9.0 %collective-permute-start = (f32[32,128]{1,0:T(8,128)S(1)}, f32[32,128]{1,0:T(8,128)S(1)}, u32[]{:S(2)}, u32[]{:S(2)}) collective-permute-start(f32[32,128]{1,0:T(8,128)S(1)} %get-tuple-element.712), channel_id=1, source_target_pairs={{0,32},{32,0},{64,96},{96,64},{128,160},{160,128},{192,224},{224,1... | collective-permute-start | bytes 49160 | tf_op jit(solution)/shard_map/while/body/eval_jaxpr/ppermute | solution.py:325
  82.7 7.5 %collective-permute-start.1 = (f32[32,128]{1,0:T(8,128)S(1)}, f32[32,128]{1,0:T(8,128)S(1)}, u32[]{:S(2)}, u32[]{:S(2)}) collective-permute-start(f32[32,128]{1,0:T(8,128)S(1)} %get-tuple-element.713), channel_id=1, source_target_pairs={{0,224},{32,64},{64,32},{96,128},{128,96},{160,192},{192,160},{224... | collective-permute-start | bytes 49160 | tf_op jit(solution)/shard_map/while/body/eval_jaxpr/ppermute | solution.py:325
  85.5 4.6 %collective-permute-start.3 = (f32[16,128]{1,0:T(8,128)S(1)}, f32[16,128]{1,0:T(8,128)S(1)}, u32[]{:S(2)}, u32[]{:S(2)}) collective-permute-start(f32[16,128]{1,0:T(8,128)S(1)} %get-tuple-element.715), channel_id=1, source_target_pairs={{0,24},{8,16},{16,8},{24,0},{1,25},{9,17},{17,9},{25,1},{2,26},{10... | collective-permute-start | bytes 24584 | tf_op jit(solution)/shard_map/while/body/eval_jaxpr/ppermute | solution.py:325
  92.0 22.4 %all-to-all-start.1 = ((f32[256,1,128]{2,1,0:T(1,128)}), f32[256,1,128]{2,1,0:T(1,128)S(1)}, u32[]{:S(2)}, u32[]{:S(2)}) async-start(f32[256,1,128]{2,1,0:T(1,128)} %bitcast.49), calls=%async_computation.1 | async-start | bytes 262144 | tf_op jit(solution)/shard_map/while/body/eval_jaxpr/all_to_all | solution.py:330
  101.7 8.0 %collective-permute-start.8 = (f32[16,128]{1,0:T(8,128)S(1)}, f32[16,128]{1,0:T(8,128)S(1)}, u32[]{:S(2)}, u32[]{:S(2)}) collective-permute-start(f32[16,128]{1,0:T(8,128)S(1)} %get-tuple-element.655), channel_id=1, source_target_pairs={{0,8},{8,0},{16,24},{24,16},{1,9},{9,1},{17,25},{25,17},{2,10},{10... | collective-permute-start | bytes 24584 | tf_op jit(solution)/shard_map/while/body/eval_jaxpr/ppermute | solution.py:325
  101.9 12.4 %collective-permute-start.10 = (f32[32,128]{1,0:T(8,128)S(1)}, f32[32,128]{1,0:T(8,128)S(1)}, u32[]{:S(2)}, u32[]{:S(2)}) collective-permute-start(f32[32,128]{1,0:T(8,128)S(1)} %get-tuple-element.657), channel_id=1, source_target_pairs={{0,1},{1,0},{2,3},{3,2},{4,5},{5,4},{6,7},{7,6},{8,9},{9,8},{10,11... | collective-permute-start | bytes 49160 | tf_op jit(solution)/shard_map/while/body/eval_jaxpr/ppermute | solution.py:325
  103.9 10.4 %collective-permute-start.11 = (f32[32,128]{1,0:T(8,128)S(1)}, f32[32,128]{1,0:T(8,128)S(1)}, u32[]{:S(2)}, u32[]{:S(2)}) collective-permute-start(f32[32,128]{1,0:T(8,128)S(1)} %get-tuple-element.657), channel_id=1, source_target_pairs={{0,7},{1,2},{2,1},{3,4},{4,3},{5,6},{6,5},{7,0},{8,15},{9,10},{10,... | collective-permute-start | bytes 49160 | tf_op jit(solution)/shard_map/while/body/eval_jaxpr/ppermute | solution.py:325
  105.4 9.0 %collective-permute-start.6 = (f32[32,128]{1,0:T(8,128)S(1)}, f32[32,128]{1,0:T(8,128)S(1)}, u32[]{:S(2)}, u32[]{:S(2)}) collective-permute-start(f32[32,128]{1,0:T(8,128)S(1)} %get-tuple-element.653), channel_id=1, source_target_pairs={{0,32},{32,0},{64,96},{96,64},{128,160},{160,128},{192,224},{224,1... | collective-permute-start | bytes 49160 | tf_op jit(solution)/shard_map/while/body/eval_jaxpr/ppermute | solution.py:325
  106.9 7.5 %collective-permute-start.7 = (f32[32,128]{1,0:T(8,128)S(1)}, f32[32,128]{1,0:T(8,128)S(1)}, u32[]{:S(2)}, u32[]{:S(2)}) collective-permute-start(f32[32,128]{1,0:T(8,128)S(1)} %get-tuple-element.654), channel_id=1, source_target_pairs={{0,224},{32,64},{64,32},{96,128},{128,96},{160,192},{192,160},{224... | collective-permute-start | bytes 49160 | tf_op jit(solution)/shard_map/while/body/eval_jaxpr/ppermute | solution.py:325
  109.7 4.6 %collective-permute-start.9 = (f32[16,128]{1,0:T(8,128)S(1)}, f32[16,128]{1,0:T(8,128)S(1)}, u32[]{:S(2)}, u32[]{:S(2)}) collective-permute-start(f32[16,128]{1,0:T(8,128)S(1)} %get-tuple-element.656), channel_id=1, source_target_pairs={{0,24},{8,16},{16,8},{24,0},{1,25},{9,17},{17,9},{25,1},{2,26},{10... | collective-permute-start | bytes 24584 | tf_op jit(solution)/shard_map/while/body/eval_jaxpr/ppermute | solution.py:325
  116.3 22.4 %all-to-all-start = ((f32[256,1,128]{2,1,0:T(1,128)}), f32[256,1,128]{2,1,0:T(1,128)S(1)}, u32[]{:S(2)}, u32[]{:S(2)}) async-start(f32[256,1,128]{2,1,0:T(1,128)} %bitcast.47), calls=%async_computation | async-start | bytes 262144 | tf_op jit(solution)/shard_map/while/body/eval_jaxpr/all_to_all | solution.py:330
  126.0 8.0 %collective-permute-start.2 = (f32[16,128]{1,0:T(8,128)S(1)}, f32[16,128]{1,0:T(8,128)S(1)}, u32[]{:S(2)}, u32[]{:S(2)}) collective-permute-start(f32[16,128]{1,0:T(8,128)S(1)} %get-tuple-element.714), channel_id=1, source_target_pairs={{0,8},{8,0},{16,24},{24,16},{1,9},{9,1},{17,25},{25,17},{2,10},{10... | collective-permute-start | bytes 24584 | tf_op jit(solution)/shard_map/while/body/eval_jaxpr/ppermute | solution.py:325
  126.2 12.4 %collective-permute-start.4 = (f32[32,128]{1,0:T(8,128)S(1)}, f32[32,128]{1,0:T(8,128)S(1)}, u32[]{:S(2)}, u32[]{:S(2)}) collective-permute-start(f32[32,128]{1,0:T(8,128)S(1)} %get-tuple-element.716), channel_id=1, source_target_pairs={{0,1},{1,0},{2,3},{3,2},{4,5},{5,4},{6,7},{7,6},{8,9},{9,8},{10,11... | collective-permute-start | bytes 49160 | tf_op jit(solution)/shard_map/while/body/eval_jaxpr/ppermute | solution.py:325
  128.2 10.4 %collective-permute-start.5 = (f32[32,128]{1,0:T(8,128)S(1)}, f32[32,128]{1,0:T(8,128)S(1)}, u32[]{:S(2)}, u32[]{:S(2)}) collective-permute-start(f32[32,128]{1,0:T(8,128)S(1)} %get-tuple-element.716), channel_id=1, source_target_pairs={{0,7},{1,2},{2,1},{3,4},{4,3},{5,6},{6,5},{7,0},{8,15},{9,10},{10,... | collective-permute-start | bytes 49160 | tf_op jit(solution)/shard_map/while/body/eval_jaxpr/ppermute | solution.py:325
  129.6 9.0 %collective-permute-start = (f32[32,128]{1,0:T(8,128)S(1)}, f32[32,128]{1,0:T(8,128)S(1)}, u32[]{:S(2)}, u32[]{:S(2)}) collective-permute-start(f32[32,128]{1,0:T(8,128)S(1)} %get-tuple-element.712), channel_id=1, source_target_pairs={{0,32},{32,0},{64,96},{96,64},{128,160},{160,128},{192,224},{224,1... | collective-permute-start | bytes 49160 | tf_op jit(solution)/shard_map/while/body/eval_jaxpr/ppermute | solution.py:325
  131.1 7.5 %collective-permute-start.1 = (f32[32,128]{1,0:T(8,128)S(1)}, f32[32,128]{1,0:T(8,128)S(1)}, u32[]{:S(2)}, u32[]{:S(2)}) collective-permute-start(f32[32,128]{1,0:T(8,128)S(1)} %get-tuple-element.713), channel_id=1, source_target_pairs={{0,224},{32,64},{64,32},{96,128},{128,96},{160,192},{192,160},{224... | collective-permute-start | bytes 49160 | tf_op jit(solution)/shard_map/while/body/eval_jaxpr/ppermute | solution.py:325
  134.0 4.6 %collective-permute-start.3 = (f32[16,128]{1,0:T(8,128)S(1)}, f32[16,128]{1,0:T(8,128)S(1)}, u32[]{:S(2)}, u32[]{:S(2)}) collective-permute-start(f32[16,128]{1,0:T(8,128)S(1)} %get-tuple-element.715), channel_id=1, source_target_pairs={{0,24},{8,16},{16,8},{24,0},{1,25},{9,17},{17,9},{25,1},{2,26},{10... | collective-permute-start | bytes 24584 | tf_op jit(solution)/shard_map/while/body/eval_jaxpr/ppermute | solution.py:325
  140.5 22.4 %all-to-all-start.1 = ((f32[256,1,128]{2,1,0:T(1,128)}), f32[256,1,128]{2,1,0:T(1,128)S(1)}, u32[]{:S(2)}, u32[]{:S(2)}) async-start(f32[256,1,128]{2,1,0:T(1,128)} %bitcast.49), calls=%async_computation.1 | async-start | bytes 262144 | tf_op jit(solution)/shard_map/while/body/eval_jaxpr/all_to_all | solution.py:330
  150.2 8.0 %collective-permute-start.8 = (f32[16,128]{1,0:T(8,128)S(1)}, f32[16,128]{1,0:T(8,128)S(1)}, u32[]{:S(2)}, u32[]{:S(2)}) collective-permute-start(f32[16,128]{1,0:T(8,128)S(1)} %get-tuple-element.655), channel_id=1, source_target_pairs={{0,8},{8,0},{16,24},{24,16},{1,9},{9,1},{17,25},{25,17},{2,10},{10... | collective-permute-start | bytes 24584 | tf_op jit(solution)/shard_map/while/body/eval_jaxpr/ppermute | solution.py:325
  150.4 12.4 %collective-permute-start.10 = (f32[32,128]{1,0:T(8,128)S(1)}, f32[32,128]{1,0:T(8,128)S(1)}, u32[]{:S(2)}, u32[]{:S(2)}) collective-permute-start(f32[32,128]{1,0:T(8,128)S(1)} %get-tuple-element.657), channel_id=1, source_target_pairs={{0,1},{1,0},{2,3},{3,2},{4,5},{5,4},{6,7},{7,6},{8,9},{9,8},{10,11... | collective-permute-start | bytes 49160 | tf_op jit(solution)/shard_map/while/body/eval_jaxpr/ppermute | solution.py:325
  152.4 10.4 %collective-permute-start.11 = (f32[32,128]{1,0:T(8,128)S(1)}, f32[32,128]{1,0:T(8,128)S(1)}, u32[]{:S(2)}, u32[]{:S(2)}) collective-permute-start(f32[32,128]{1,0:T(8,128)S(1)} %get-tuple-element.657), channel_id=1, source_target_pairs={{0,7},{1,2},{2,1},{3,4},{4,3},{5,6},{6,5},{7,0},{8,15},{9,10},{10,... | collective-permute-start | bytes 49160 | tf_op jit(solution)/shard_map/while/body/eval_jaxpr/ppermute | solution.py:325
  153.8 9.0 %collective-permute-start.6 = (f32[32,128]{1,0:T(8,128)S(1)}, f32[32,128]{1,0:T(8,128)S(1)}, u32[]{:S(2)}, u32[]{:S(2)}) collective-permute-start(f32[32,128]{1,0:T(8,128)S(1)} %get-tuple-element.653), channel_id=1, source_target_pairs={{0,32},{32,0},{64,96},{96,64},{128,160},{160,128},{192,224},{224,1... | collective-permute-start | bytes 49160 | tf_op jit(solution)/shard_map/while/body/eval_jaxpr/ppermute | solution.py:325
  155.3 7.5 %collective-permute-start.7 = (f32[32,128]{1,0:T(8,128)S(1)}, f32[32,128]{1,0:T(8,128)S(1)}, u32[]{:S(2)}, u32[]{:S(2)}) collective-permute-start(f32[32,128]{1,0:T(8,128)S(1)} %get-tuple-element.654), channel_id=1, source_target_pairs={{0,224},{32,64},{64,32},{96,128},{128,96},{160,192},{192,160},{224... | collective-permute-start | bytes 49160 | tf_op jit(solution)/shard_map/while/body/eval_jaxpr/ppermute | solution.py:325
  158.2 4.6 %collective-permute-start.9 = (f32[16,128]{1,0:T(8,128)S(1)}, f32[16,128]{1,0:T(8,128)S(1)}, u32[]{:S(2)}, u32[]{:S(2)}) collective-permute-start(f32[16,128]{1,0:T(8,128)S(1)} %get-tuple-element.656), channel_id=1, source_target_pairs={{0,24},{8,16},{16,8},{24,0},{1,25},{9,17},{17,9},{25,1},{2,26},{10... | collective-permute-start | bytes 24584 | tf_op jit(solution)/shard_map/while/body/eval_jaxpr/ppermute | solution.py:325
  164.7 22.4 %all-to-all-start.2 = ((f32[256,1,128]{2,1,0:T(1,128)}), f32[256,1,128]{2,1,0:T(1,128)S(1)}, u32[]{:S(2)}, u32[]{:S(2)}) async-start(f32[256,1,128]{2,1,0:T(1,128)} %bitcast.48), calls=%async_computation.2 | async-start | bytes 262144 | tf_op jit(solution)/shard_map/all_to_all | solution.py:330
  174.4 8.0 %collective-permute-start.20 = (f32[16,128]{1,0:T(8,128)S(1)}, f32[16,128]{1,0:T(8,128)S(1)}, u32[]{:S(2)}, u32[]{:S(2)}) collective-permute-start(f32[16,128]{1,0:T(8,128)S(1)} %get-tuple-element.434), channel_id=1, source_target_pairs={{0,8},{8,0},{16,24},{24,16},{1,9},{9,1},{17,25},{25,17},{2,10},{10... | collective-permute-start | bytes 24584 | tf_op jit(solution)/shard_map/ppermute | solution.py:325
  174.6 12.4 %collective-permute-start.22 = (f32[32,128]{1,0:T(8,128)S(1)}, f32[32,128]{1,0:T(8,128)S(1)}, u32[]{:S(2)}, u32[]{:S(2)}) collective-permute-start(f32[32,128]{1,0:T(8,128)S(1)} %get-tuple-element.436), channel_id=1, source_target_pairs={{0,1},{1,0},{2,3},{3,2},{4,5},{5,4},{6,7},{7,6},{8,9},{9,8},{10,11... | collective-permute-start | bytes 49160 | tf_op jit(solution)/shard_map/ppermute | solution.py:325
  176.6 10.4 %collective-permute-start.23 = (f32[32,128]{1,0:T(8,128)S(1)}, f32[32,128]{1,0:T(8,128)S(1)}, u32[]{:S(2)}, u32[]{:S(2)}) collective-permute-start(f32[32,128]{1,0:T(8,128)S(1)} %get-tuple-element.436), channel_id=1, source_target_pairs={{0,7},{1,2},{2,1},{3,4},{4,3},{5,6},{6,5},{7,0},{8,15},{9,10},{10,... | collective-permute-start | bytes 49160 | tf_op jit(solution)/shard_map/ppermute | solution.py:325
  178.1 9.0 %collective-permute-start.18 = (f32[32,128]{1,0:T(8,128)S(1)}, f32[32,128]{1,0:T(8,128)S(1)}, u32[]{:S(2)}, u32[]{:S(2)}) collective-permute-start(f32[32,128]{1,0:T(8,128)S(1)} %get-tuple-element.432), channel_id=1, source_target_pairs={{0,32},{32,0},{64,96},{96,64},{128,160},{160,128},{192,224},{224,1... | collective-permute-start | bytes 49160 | tf_op jit(solution)/shard_map/ppermute | solution.py:325
  179.6 7.5 %collective-permute-start.19 = (f32[32,128]{1,0:T(8,128)S(1)}, f32[32,128]{1,0:T(8,128)S(1)}, u32[]{:S(2)}, u32[]{:S(2)}) collective-permute-start(f32[32,128]{1,0:T(8,128)S(1)} %get-tuple-element.433), channel_id=1, source_target_pairs={{0,224},{32,64},{64,32},{96,128},{128,96},{160,192},{192,160},{224... | collective-permute-start | bytes 49160 | tf_op jit(solution)/shard_map/ppermute | solution.py:325
  182.4 4.6 %collective-permute-start.21 = (f32[16,128]{1,0:T(8,128)S(1)}, f32[16,128]{1,0:T(8,128)S(1)}, u32[]{:S(2)}, u32[]{:S(2)}) collective-permute-start(f32[16,128]{1,0:T(8,128)S(1)} %get-tuple-element.435), channel_id=1, source_target_pairs={{0,24},{8,16},{16,8},{24,0},{1,25},{9,17},{17,9},{25,1},{2,26},{10... | collective-permute-start | bytes 24584 | tf_op jit(solution)/shard_map/ppermute | solution.py:325
  212.7 18.7 %all-to-all-start.4 = ((f32[256,1,128]{2,1,0:T(1,128)}), f32[256,1,128]{2,1,0:T(1,128)S(1)}, u32[]{:S(2)}, u32[]{:S(2)}) async-start(f32[256,1,128]{2,1,0:T(1,128)} %bitcast.20), calls=%async_computation.4 | async-start | bytes 262144 | tf_op jit(solution)/shard_map/all_to_all | solution.py:330
